TPU v7x, 128 devices: a whole 4x4x4 slice. The times are simulated.
128 devices in a mesh: row: 16 (over x_hi, z, core), col: 8 (over y, x_lo).
Axes of the slice: x: 4 (x_hi: 2, x_lo: 2; x = x_hi * 2 + x_lo), y: 4, z: 4, core: 2. Of those that a mesh axis runs over, the one named last changes fastest.
Arguments:
- spins_up: int32 [10240, 16384], P('row', 'col'), may hold values from 0 to 1
- uniforms: float32 [2, 10240, 16384], P(None, 'row', 'col'), may hold values from 0 to 1
- moments: bfloat16 [10240, 16384], P('row', 'col'), may hold values from 0.5 to 2
- accept_bar: float32 [2], replicated, may hold values from 0.06 to 0.6, as said below
Outputs:
- spins_out: float32 [10240, 16384], P('row', 'col')
- corr: float32 [2048], P(('row', 'col'))
Inputs may be any that keep to these rules, and one draw needn't show every extreme that they name: accept_bar[1] equals accept_bar[0] squared, as exp(-8 beta) and exp(-4 beta) for one inverse temperature beta of the draw.
All inputs are finite; a program needn't handle non-finite values.
Results may differ from a plain program's by a relative error of at most 0.0003.
Values may be sent and summed in bfloat16 or wider, within the bound.
A program may use at most 128 MiB of HBM per device.

v0:
```python
import math

import jax
import jax.numpy as jnp
from jax import lax
from jax.sharding import PartitionSpec as P

R = 2048
SWEEPS = 2


def with_halo(value, sides, width):
    for axis, dim in sides:
        count, length = (lax.axis_size(axis), value.shape[dim])
        up = [(i, (i + 1) % count) for i in range(count)]
        down = [(j, i) for i, j in up]
        last = lax.slice_in_dim(value, length - width, length, axis=dim)
        leading = lax.slice_in_dim(value, 0, width, axis=dim)
        before = lax.ppermute(last, axis, up)
        after = lax.ppermute(leading, axis, down)
        value = jnp.concatenate([before, value, after], axis=dim)
    return value


def update_colour(padded, uniform_draws, accept_bar, colour):
    centre = padded[1:-1, 1:-1]
    neighbours = padded[2:, 1:-1] + padded[:-2, 1:-1] + padded[1:-1, 2:] + padded[1:-1, :-2]
    alignment = centre * neighbours
    threshold = jnp.where(alignment > 3.0, accept_bar[1], accept_bar[0])
    row_ids = lax.broadcasted_iota(jnp.int32, centre.shape, 0)
    col_ids = lax.broadcasted_iota(jnp.int32, centre.shape, 1)
    coloured = (row_ids + col_ids) % 2 == colour
    flipped = coloured & ((alignment <= 0.0) | (uniform_draws < threshold))
    return jnp.where(flipped, -centre, centre)


def correlate(left_cells, right_cells, max_distance, tile_width):
    row_count = left_cells.shape[0]
    tile_count = left_cells.shape[1] // tile_width
    offsets = max_distance // tile_width
    left_tiles = left_cells.reshape(row_count, tile_count, tile_width)
    right_tiles = right_cells.reshape(row_count, tile_count + offsets, tile_width)

    def product(offset):
        shifted = lax.dynamic_slice_in_dim(right_tiles, offset, tile_count, 1)
        return jnp.einsum("itp,itq->pq", left_tiles, shifted, preferred_element_type=jnp.float32)

    products = lax.map(product, jnp.arange(offsets + 1, dtype=jnp.int32))
    paired = jnp.concatenate([products[:-1], products[1:]], axis=2)
    flattened = paired.reshape(offsets, tile_width * 2 * tile_width)
    flattened = jnp.pad(flattened, ((0, 0), (0, tile_width)))
    skewed = flattened.reshape(offsets, tile_width, 2 * tile_width + 1)[:, :, :tile_width]
    return jnp.sum(skewed, axis=1).reshape(max_distance)


def on_device(spins_up, uniforms, moments, accept_bar):
    lattice = (2 * spins_up - 1).astype(jnp.float32)
    wide_draws = with_halo(uniforms, (("row", 1), ("col", 2)), 1)
    for sweep_index in range(SWEEPS):
        padded = with_halo(lattice.astype(jnp.bfloat16), (("row", 0), ("col", 1)), 2).astype(
            lattice.dtype
        )
        middle = update_colour(padded, wide_draws[sweep_index], accept_bar, 0)
        lattice = update_colour(middle, uniforms[sweep_index], accept_bar, 1)
    weighted = moments * lattice.astype(jnp.bfloat16)
    columns = weighted.shape[1]
    tile_width = 128
    full_rows = lax.all_to_all(weighted, "col", split_axis=0, concat_axis=1, tiled=True)
    extended = jnp.concatenate([full_rows, full_rows[:, :R]], axis=1)
    partial_sums = correlate(full_rows, extended, R, tile_width)
    row_devices = lax.axis_size("row")
    col_devices = lax.axis_size("col")
    normaliser = 1.0 / math.sqrt(lattice.shape[0] * row_devices * columns * col_devices)
    owned_sums = lax.psum_scatter(partial_sums, ("row", "col"), scatter_dimension=0, tiled=True)
    return (lattice, owned_sums * normaliser)


def solution(mesh):
    placed = (P("row", "col"), P(None, "row", "col"), P("row", "col"), P())
    return jax.shard_map(
        on_device,
        mesh=mesh,
        in_specs=placed,
        out_specs=(P("row", "col"), P(("row", "col"))),
        check_vma=False,
    )
```

profile of v0, /device:TPU:0, one launch (start us, length us, event | category | flops | bytes accessed | tf_op | source)
XLA Modules:
  0.0 357.0 jit_solution(10594894259749702739)
XLA Ops:
  3.9 6.1 %collective-permute-start.1 = (bf16[2,2048]{1,0:T(2,128)(2,1)S(1)}, bf16[2,2048]{1,0:T(2,128)(2,1)S(1)}, u32[]{:S(2)}, u32[]{:S(2)}) collective-permute-start(bf16[2,2048]{1,0:T(2,128)(2,1)S(1)} %get-tuple-element.70), channel_id=1, source_target_pairs={{8,0},{16,8},{24,16},{32,24},{40,32},{48,40},{56,48},{64,56},{72,6... | collective-permute-start | bytes 24584 | tf_op jit(solution)/shard_map/ppermute | solution.py:20
  11.0 5.4 %collective-permute-start.5 = (f32[2,1,2048]{2,1,0:T(1,128)S(1)}, f32[2,1,2048]{2,1,0:T(1,128)S(1)}, u32[]{:S(2)}, u32[]{:S(2)}) collective-permute-start(f32[2,1,2048]{2,1,0:T(1,128)S(1)} %get-tuple-element.62), channel_id=1, source_target_pairs={{8,0},{16,8},{24,16},{32,24},{40,32},{48,40},{56,48},{64,56},{72,6... | collective-permute-start | bytes 49160 | tf_op jit(solution)/shard_map/ppermute | solution.py:20
  18.8 3.5 collective-permute-start.3
  23.3 5.3 %pad_maximum_fusion = f32[2,642,2048]{2,1,0:T(8,128)S(1)} fusion(f32[2,1,2048]{2,1,0:T(1,128)S(1)} %collective-permute-done.5, f32[2,640,2048]{2,1,0:T(8,128)} %param.7, f32[2,1,2048]{2,1,0:T(1,128)S(1)} %collective-permute-done.4), kind=kLoop, calls=%fused_computation.5 | loop fusion | flops 5259264 | bytes 21037056 | tf_op jit(solution)/shard_map/concatenate | solution.py:21
  28.6 3.9 %copy-done = f32[2,642,2048]{2,1,0:T(8,128)} copy-done((f32[2,642,2048]{2,1,0:T(8,128)}, f32[2,642,2048]{2,1,0:T(8,128)S(1)}, u32[]{:S(2)}) %copy-start) | copy-done | bytes 10518552
  35.9 3.7 %collective-permute-start.7 = (f32[2,642,1]{1,0,2:T(2,128)S(1)}, f32[2,642,1]{1,0,2:T(2,128)S(1)}, u32[]{:S(2)}, u32[]{:S(2)}) collective-permute-start(f32[2,642,1]{1,0,2:T(2,128)S(1)} %copy.24), channel_id=1, source_target_pairs={{1,0},{2,1},{3,2},{4,3},{5,4},{6,5},{7,6},{0,7},{9,8},{10,9},{11,1... | collective-permute-start | bytes 15416 | tf_op jit(solution)/shard_map/ppermute | solution.py:20
  40.2 5.3 %concatenate.25 = bf16[644,2052]{1,0:T(8,128)(2,1)} concatenate(bf16[644,2]{1,0:T(8,128)(2,1)S(1)} %collective-permute-done.2, bf16[644,2048]{1,0:T(8,128)(2,1)S(1)} %pad_maximum_fusion.1, bf16[644,2]{1,0:T(8,128)(2,1)} %collective-permute-done.3), dimensions={1} | concatenate | bytes 5285952 | tf_op jit(solution)/shard_map/concatenate | solution.py:21
  45.5 4.7 %convert_element_type.22 = f32[644,2052]{1,0:T(8,128)} convert(bf16[644,2052]{1,0:T(8,128)(2,1)} %concatenate.25) | non-fusion elementwise | flops 1321488 | bytes 7928928 | tf_op jit(solution)/shard_map/convert_element_type | solution.py:60
  50.8 13.9 %concatenate.27 = f32[2,642,2050]{2,1,0:T(8,128)} concatenate(f32[2,642,1]{2,1,0:T(8,128)S(1)} %copy.25, f32[2,642,2048]{2,1,0:T(8,128)} %copy-done, f32[2,642,1]{2,1,0:T(8,128)S(1)} %copy.26), dimensions={2} | concatenate | bytes 21057600 | tf_op jit(solution)/shard_map/concatenate | solution.py:21
  64.6 20.0 %negate_select_fusion.1 = f32[642,2050]{1,0:T(8,128)S(1)} fusion(f32[2,642,2050]{2,1,0:T(8,128)} %concatenate.27, f32[644,2052]{1,0:T(8,128)} %convert_element_type.22, f32[]{:T(128)} %bitcast.6, f32[]{:T(128)} %bitcast.5), kind=kLoop, calls=%fused_computation.7 | loop fusion | flops 32902500 | bytes 36850808 | tf_op jit(solution)/shard_map/jit(_where)/select_n | solution.py:34
  84.6 10.1 %fusion.24 = bf16[640,2048]{1,0:T(8,128)(2,1)S(1)} fusion(f32[2,640,2048]{2,1,0:T(8,128)} %param.7, f32[642,2050]{1,0:T(8,128)S(1)} %negate_select_fusion.1, f32[]{:T(128)} %bitcast.6, f32[]{:T(128)} %bitcast.5), kind=kLoop, calls=%fused_computation.39 | loop fusion | flops 34078720 | bytes 34078728 | tf_op jit(solution)/shard_map/convert_element_type | solution.py:60
  99.2 5.3 %collective-permute-done.8 = bf16[2,2048]{1,0:T(2,128)(2,1)S(1)} collective-permute-done((bf16[2,2048]{1,0:T(2,128)(2,1)S(1)}, bf16[2,2048]{1,0:T(2,128)(2,1)S(1)}, u32[]{:S(2)}, u32[]{:S(2)}) %collective-permute-start.8) | collective-permute-done | bytes 8224 | tf_op jit(solution)/shard_map/ppermute | solution.py:19
  105.5 4.1 %collective-permute-start.11 = (bf16[644,2]{1,0:T(8,128)(2,1)S(1)}, bf16[644,2]{1,0:T(8,128)(2,1)S(1)}, u32[]{:S(2)}, u32[]{:S(2)}) collective-permute-start(bf16[644,2]{1,0:T(8,128)(2,1)S(1)} %get-tuple-element.63), channel_id=1, source_target_pairs={{1,0},{2,1},{3,2},{4,3},{5,4},{6,5},{7,6},{0,7},{9,8},{10,9},{11,1... | collective-permute-start | bytes 7736 | tf_op jit(solution)/shard_map/ppermute | solution.py:20
  112.9 4.4 %concatenate.29 = bf16[644,2052]{1,0:T(8,128)(2,1)} concatenate(bf16[644,2]{1,0:T(8,128)(2,1)S(1)} %collective-permute-done.10, bf16[644,2048]{1,0:T(8,128)(2,1)S(1)} %pad_maximum_fusion.2, bf16[644,2]{1,0:T(8,128)(2,1)S(1)} %collective-permute-done.11), dimensions={1} | concatenate | bytes 5285952 | tf_op jit(solution)/shard_map/concatenate | solution.py:21
  119.5 10.1 %negate_select_fusion = f32[642,2050]{1,0:T(8,128)S(1)} fusion(f32[2,642,2050]{2,1,0:T(8,128)} %concatenate.27, f32[644,2052]{1,0:T(8,128)S(1)} %convert_element_type.24, f32[]{:T(128)} %bitcast.6, f32[]{:T(128)} %bitcast.5), kind=kLoop, calls=%fused_computation.6 | loop fusion | flops 32902500 | bytes 36850808 | tf_op jit(solution)/shard_map/jit(_where)/select_n | solution.py:34
  129.6 12.4 %convert_multiply_fusion = (bf16[640,2048]{1,0:T(8,128)(2,1)}, f32[640,2048]{1,0:T(8,128)}) fusion(bf16[640,2048]{1,0:T(8,128)(2,1)S(1)} %copy-done.1, f32[]{:T(128)} %bitcast.6, f32[]{:T(128)} %bitcast.5, f32[2,640,2048]{2,1,0:T(8,128)} %param.7, f32[642,2050]{1,0:T(8,128)S(1)} %negate_select_fusion), kind=kLoop, calls=%fused_computation.61 | loop fusion | flops 39321600 | bytes 41943048 | tf_op jit(solution)/shard_map/mul | solution.py:65
  142.1 5.4 %all-to-all-start = ((bf16[8,80,2048]{2,1,0:T(8,128)(2,1)}), bf16[8,80,2048]{2,1,0:T(8,128)(2,1)S(1)}, u32[]{:S(2)}, u32[]{:S(2)}) async-start(bf16[8,80,2048]{2,1,0:T(8,128)(2,1)} %bitcast.71), calls=%async_computation | async-start | bytes 5242880 | tf_op jit(solution)/shard_map/all_to_all | solution.py:68
  147.5 25.9 %all-to-all-done = bf16[8,80,2048]{2,1,0:T(8,128)(2,1)S(1)} async-done(((bf16[8,80,2048]{2,1,0:T(8,128)(2,1)}), bf16[8,80,2048]{2,1,0:T(8,128)(2,1)S(1)}, u32[]{:S(2)}, u32[]{:S(2)}) %all-to-all-start) | async-done | bytes 2621472 | tf_op jit(solution)/shard_map/all_to_all | solution.py:68
  178.8 3.9 %reshape.24 = bf16[80,128,128]{2,1,0:T(8,128)(2,1)S(1)} reshape(bf16[80,8,2048]{2,1,0:T(8,128)(2,1)} %copy.27) | data formatting | bytes 5242880 | tf_op jit(solution)/shard_map/reshape | solution.py:41
  182.6 100.2 %while.10 = (s32[]{:T(128)}, f32[17,128,128]{1,2,0:T(8,128)}, s32[17]{0:T(128)S(1)}, bf16[80,144,128]{2,1,0:T(8,128)(2,1)}, bf16[80,128,128]{2,1,0:T(8,128)(2,1)S(1)}, /*index=5*/s32[]{:T(128)}, s32[]{:T(128)}, s32[]{:T(128)}) while((s32[]{:T(128)}, f32[17,128,128]{1,2,0:T(8,128)}, s32[17]{0:T(128)S(1)}, bf16[80,144,128]{2,1,0:T(8,128)(2,1)}, ...), condition=%wide.region_1.2_spmd, body=%wide.region_0.1_spmd.sunk | while | flops 335544320 | bytes 5308563 | solution.py:48
  197.0 3.4 fusion.48
  273.6 3.4 fusion.48
  288.4 3.6 %reshape.26 = f32[16,128,257]{2,1,0:T(8,128)} reshape(f32[16,32896]{1,0:T(8,128)S(1)} %pad.4) | data formatting | bytes 4210688 | tf_op jit(solution)/shard_map/reshape | solution.py:52
  293.3 63.1 %all-reduce.1 = f32[2048]{0:T(1024)S(1)} all-reduce(f32[2048]{0:T(1024)S(1)} %bitcast.74), channel_id=2, replica_groups=mesh['row'=16,'col'=8] {'row','col'}, use_global_device_ids=true, to_apply=%region_3.4.clone | all-reduce | flops 2048 | bytes 16384
  (83 shorter events, 97.1 us)
Async XLA Ops:
  3.9 12.5 %collective-permute-start.1 = (bf16[2,2048]{1,0:T(2,128)(2,1)S(1)}, bf16[2,2048]{1,0:T(2,128)(2,1)S(1)}, u32[]{:S(2)}, u32[]{:S(2)}) collective-permute-start(bf16[2,2048]{1,0:T(2,128)(2,1)S(1)} %get-tuple-element.70), channel_id=1, source_target_pairs={{8,0},{16,8},{24,16},{32,24},{40,32},{48,40},{56,48},{64,56},{72,6... | collective-permute-start | bytes 24584 | tf_op jit(solution)/shard_map/ppermute | solution.py:20
  10.0 6.7 %collective-permute-start = (bf16[2,2048]{1,0:T(2,128)(2,1)S(1)}, bf16[2,2048]{1,0:T(2,128)(2,1)S(1)}, u32[]{:S(2)}, u32[]{:S(2)}) collective-permute-start(bf16[2,2048]{1,0:T(2,128)(2,1)S(1)} %get-tuple-element.69), channel_id=1, source_target_pairs={{0,8},{8,16},{16,24},{24,32},{32,40},{40,48},{48,56},{56,64},{64,7... | collective-permute-start | bytes 24584 | tf_op jit(solution)/shard_map/ppermute | solution.py:19
  11.0 11.4 %collective-permute-start.5 = (f32[2,1,2048]{2,1,0:T(1,128)S(1)}, f32[2,1,2048]{2,1,0:T(1,128)S(1)}, u32[]{:S(2)}, u32[]{:S(2)}) collective-permute-start(f32[2,1,2048]{2,1,0:T(1,128)S(1)} %get-tuple-element.62), channel_id=1, source_target_pairs={{8,0},{16,8},{24,16},{32,24},{40,32},{48,40},{56,48},{64,56},{72,6... | collective-permute-start | bytes 49160 | tf_op jit(solution)/shard_map/ppermute | solution.py:20
  16.4 6.9 %collective-permute-start.4 = (f32[2,1,2048]{2,1,0:T(1,128)S(1)}, f32[2,1,2048]{2,1,0:T(1,128)S(1)}, u32[]{:S(2)}, u32[]{:S(2)}) collective-permute-start(f32[2,1,2048]{2,1,0:T(1,128)S(1)} %get-tuple-element.61), channel_id=1, source_target_pairs={{0,8},{8,16},{16,24},{24,32},{32,40},{40,48},{48,56},{56,64},{64,7... | collective-permute-start | bytes 49160 | tf_op jit(solution)/shard_map/ppermute | solution.py:19
  18.2 22.0 %collective-permute-start.2 = (bf16[644,2]{1,0:T(8,128)(2,1)}, bf16[644,2]{1,0:T(8,128)(2,1)S(1)}, u32[]{:S(2)}, u32[]{:S(2)}) collective-permute-start(bf16[644,2]{1,0:T(8,128)(2,1)} %get-tuple-element.66), channel_id=1, source_target_pairs={{0,1},{1,2},{2,3},{3,4},{4,5},{5,6},{6,7},{7,0},{8,9},{9,10},{10,1... | collective-permute-start | bytes 7736 | tf_op jit(solution)/shard_map/ppermute | solution.py:19
  18.8 20.8 %copy-start.2 = (f32[2]{0:T(128)S(1)}, f32[2]{0:T(128)}, u32[]{:S(2)}) copy-start(f32[2]{0:T(128)} %param.9) | copy-start | bytes 28
  18.8 21.4 %collective-permute-start.3 = (bf16[644,2]{1,0:T(8,128)(2,1)}, bf16[644,2]{1,0:T(8,128)(2,1)}, u32[]{:S(2)}, u32[]{:S(2)}) collective-permute-start(bf16[644,2]{1,0:T(8,128)(2,1)} %get-tuple-element.65), channel_id=1, source_target_pairs={{1,0},{2,1},{3,2},{4,3},{5,4},{6,5},{7,6},{0,7},{9,8},{10,9},{11,1... | collective-permute-start | bytes 7736 | tf_op jit(solution)/shard_map/ppermute | solution.py:20
  28.6 3.9 %copy-start = (f32[2,642,2048]{2,1,0:T(8,128)}, f32[2,642,2048]{2,1,0:T(8,128)S(1)}, u32[]{:S(2)}) copy-start(f32[2,642,2048]{2,1,0:T(8,128)S(1)} %pad_maximum_fusion) | copy-start | bytes 31555588
  35.0 15.2 %collective-permute-start.6 = (f32[2,642,1]{1,0,2:T(2,128)S(1)}, f32[2,642,1]{1,0,2:T(2,128)S(1)}, u32[]{:S(2)}, u32[]{:S(2)}) collective-permute-start(f32[2,642,1]{1,0,2:T(2,128)S(1)} %copy.23), channel_id=1, source_target_pairs={{0,1},{1,2},{2,3},{3,4},{4,5},{5,6},{6,7},{7,0},{8,9},{9,10},{10,1... | collective-permute-start | bytes 15416 | tf_op jit(solution)/shard_map/ppermute | solution.py:19
  35.9 14.6 %collective-permute-start.7 = (f32[2,642,1]{1,0,2:T(2,128)S(1)}, f32[2,642,1]{1,0,2:T(2,128)S(1)}, u32[]{:S(2)}, u32[]{:S(2)}) collective-permute-start(f32[2,642,1]{1,0,2:T(2,128)S(1)} %copy.24), channel_id=1, source_target_pairs={{1,0},{2,1},{3,2},{4,3},{5,4},{6,5},{7,6},{0,7},{9,8},{10,9},{11,1... | collective-permute-start | bytes 15416 | tf_op jit(solution)/shard_map/ppermute | solution.py:20
  94.8 4.4 %collective-permute-start.9 = (bf16[2,2048]{1,0:T(2,128)(2,1)S(1)}, bf16[2,2048]{1,0:T(2,128)(2,1)S(1)}, u32[]{:S(2)}, u32[]{:S(2)}) collective-permute-start(bf16[2,2048]{1,0:T(2,128)(2,1)S(1)} %get-tuple-element.68), channel_id=1, source_target_pairs={{8,0},{16,8},{24,16},{32,24},{40,32},{48,40},{56,48},{64,56},{72,6... | collective-permute-start | bytes 24584 | tf_op jit(solution)/shard_map/ppermute | solution.py:20
  97.9 6.7 %collective-permute-start.8 = (bf16[2,2048]{1,0:T(2,128)(2,1)S(1)}, bf16[2,2048]{1,0:T(2,128)(2,1)S(1)}, u32[]{:S(2)}, u32[]{:S(2)}) collective-permute-start(bf16[2,2048]{1,0:T(2,128)(2,1)S(1)} %get-tuple-element.67), channel_id=1, source_target_pairs={{0,8},{8,16},{16,24},{24,32},{32,40},{40,48},{48,56},{56,64},{64,7... | collective-permute-start | bytes 24584 | tf_op jit(solution)/shard_map/ppermute | solution.py:19
  105.4 7.5 %collective-permute-start.10 = (bf16[644,2]{1,0:T(8,128)(2,1)S(1)}, bf16[644,2]{1,0:T(8,128)(2,1)S(1)}, u32[]{:S(2)}, u32[]{:S(2)}) collective-permute-start(bf16[644,2]{1,0:T(8,128)(2,1)S(1)} %get-tuple-element.64), channel_id=1, source_target_pairs={{0,1},{1,2},{2,3},{3,4},{4,5},{5,6},{6,7},{7,0},{8,9},{9,10},{10,1... | collective-permute-start | bytes 7736 | tf_op jit(solution)/shard_map/ppermute | solution.py:19
  105.5 7.4 %collective-permute-start.11 = (bf16[644,2]{1,0:T(8,128)(2,1)S(1)}, bf16[644,2]{1,0:T(8,128)(2,1)S(1)}, u32[]{:S(2)}, u32[]{:S(2)}) collective-permute-start(bf16[644,2]{1,0:T(8,128)(2,1)S(1)} %get-tuple-element.63), channel_id=1, source_target_pairs={{1,0},{2,1},{3,2},{4,3},{5,4},{6,5},{7,6},{0,7},{9,8},{10,9},{11,1... | collective-permute-start | bytes 7736 | tf_op jit(solution)/shard_map/ppermute | solution.py:20
  119.5 10.1 %copy-start.1 = (bf16[640,2048]{1,0:T(8,128)(2,1)S(1)}, bf16[640,2048]{1,0:T(8,128)(2,1)}, u32[]{:S(2)}) copy-start(bf16[640,2048]{1,0:T(8,128)(2,1)} %param.8) | copy-start | bytes 7864324
  142.1 31.3 %all-to-all-start = ((bf16[8,80,2048]{2,1,0:T(8,128)(2,1)}), bf16[8,80,2048]{2,1,0:T(8,128)(2,1)S(1)}, u32[]{:S(2)}, u32[]{:S(2)}) async-start(bf16[8,80,2048]{2,1,0:T(8,128)(2,1)} %bitcast.71), calls=%async_computation | async-start | bytes 5242880 | tf_op jit(solution)/shard_map/all_to_all | solution.py:68
where the time goes:
time: 360 us; the launch traced here: 357 us
  other arithmetic  71.7 us (20%)
  blocking collectives  63.1 us (18%)
  local copies, waits for them, and re-layouts  62 us (17%)
  matrix products  57.3 us (16%)
  waiting for transfers between devices  37.1 us (10%)
  starting transfers between devices  32.7 us (9%)
  loops' own time  32.1 us (9%)
    unnamed x1, blocking collectives  63.1 us
    dot_general x17, matrix products, product(): jnp.einsum('itp,itq->pq', left_tiles, shifted, preferred_element_type=jnp...  57.3 us
    another operation x1, loops' own time, correlate(): products = lax.map(product, jnp.arange(offsets + 1, dtype=jnp.int32))  32.1 us
    select_n x2, other arithmetic, update_colour(): return jnp.where(flipped, -centre, centre)  30.1 us
    ppermute x6, starting transfers between devices, with_halo(): after = lax.ppermute(leading, axis, down)  26 us
    all_to_all x1, waiting for transfers between devices, on_device(): lax.all_to_all(weighted, 'col', split_axis=0, concat_axis=1, tiled=True)  25.9 us
    concatenate x3, local copies, waits for them, and re-layouts, with_halo(): value = jnp.concatenate([before, value, after], axis=dim)  23.5 us
    convert_element_type x2, other arithmetic, on_device(): lattice.astype(jnp.bfloat16)  13.4 us
  transfers between devices with their start and end apart: 13, of which 6 were waited for; matrix products, arithmetic and copies ran while one was open for 6% of the time, Pallas kernels for 0%

commit v1 on v0

v1 whole, which is shorter than its diff:
```python
import math

import jax
import jax.numpy as jnp
from jax import lax
from jax.experimental import pallas as pl
from jax.experimental.pallas import tpu as pltpu
from jax.sharding import PartitionSpec as P

ROWS = 640
CB = 2048
R = 2048
NROW = 16
NCOL = 8
HALO = 8
UNIT = 64
CHUNKS = 5
WIDE = CB + 128
TILE = 256
MESH = pl.DeviceIdType.MESH


def kernel(
    su_hbm, u_hbm, m_hbm, bar, w_hbm, corr_ref,
    su, u, m, ht, wk, wn, buf, lt, prod, fold, outbox, inbox, vb, rs1, rs2, sb,
    edge_sem, u_sem, s_sem, m_sem, w_sem, col_send, col_recv,
    row_send, row_recv, ys, yr, xs, xr, r1s, r1r, r2s, r2r,
):
    f32, bf16 = jnp.float32, jnp.bfloat16
    row = lax.axis_index("row")
    col = lax.axis_index("col")
    par = lax.rem(col, 2)
    xcol = col + 1 - 2 * par
    ycol = lax.rem(col + 6 + 4 * par, NCOL)
    left, right = lax.rem(col + NCOL - 1, NCOL), lax.rem(col + 1, NCOL)
    up, down = lax.rem(row + NROW - 1, NROW), lax.rem(row + 1, NROW)
    own = 16 * par
    far = 16 * (1 - par)

    barrier = pltpu.get_barrier_semaphore()
    for i in range(1, NROW):
        pl.semaphore_signal(
            barrier, inc=1, device_id=(lax.rem(row + i, NROW), col), device_id_type=MESH
        )
    for i in range(1, NCOL):
        pl.semaphore_signal(
            barrier, inc=1, device_id=(row, lax.rem(col + i, NCOL)), device_id_type=MESH
        )

    def edge_copies():
        out = []
        for e, lo in enumerate((0, CB - 128)):
            lanes = pl.ds(lo, 128)
            out.append(pltpu.make_async_copy(
                u_hbm.at[:, :, lanes], u.at[:, pl.ds(HALO, ROWS), lanes], edge_sem.at[2 * e]))
            out.append(pltpu.make_async_copy(
                su_hbm.at[:, lanes], su.at[pl.ds(HALO, ROWS), lanes], edge_sem.at[2 * e + 1]))
        return out

    inner = pl.ds(128, CB - 256)

    def piece_copies(j):
        at = pl.multiple_of(j * UNIT, UNIT)
        to = pl.multiple_of(j * UNIT + HALO, 8)
        return (
            pltpu.make_async_copy(
                u_hbm.at[:, pl.ds(at, UNIT), inner], u.at[:, pl.ds(to, UNIT), inner], u_sem.at[j]),
            pltpu.make_async_copy(
                su_hbm.at[pl.ds(at, UNIT), inner], su.at[pl.ds(to, UNIT), inner], s_sem.at[j]),
            pltpu.make_async_copy(
                m_hbm.at[pl.ds(at, UNIT), :], m.at[pl.ds(at, UNIT), :], m_sem.at[j]),
        )

    for cp in edge_copies():
        cp.start()
    for j in (4, 3, 5):
        for cp in piece_copies(j):
            cp.start()

    a0 = bar[0]
    a1 = bar[1]

    def limit(draws):
        return jnp.where(draws < a1, 4.0, jnp.where(draws < a0, 2.0, 0.0)).astype(f32)

    def select(side, k):
        r = lax.broadcasted_iota(jnp.int32, (16, 128), 0)
        c = lax.broadcasted_iota(jnp.int32, (16, 128), 1)
        c = c - 124 * side
        hit = (c >= 0) & (c < 4) & (r == 4 * k + c)
        return jnp.where(hit, 1.0, 0.0).astype(bf16)

    wk[0:8, :] = jnp.zeros((8, WIDE), f32)
    wk[88:96, :] = jnp.zeros((8, WIDE), f32)
    for cp in edge_copies():
        cp.wait()

    def pack_edges(b, carry):
        r = pl.multiple_of(HALO + 128 * b, 8)
        dst = pl.ds(pl.multiple_of(128 * b, 128), 128)
        for side in range(2):
            lanes = pl.ds(side * (CB - 128), 128)
            parts = (
                (2 * su[pl.ds(r, 128), lanes] - 1).astype(f32),
                limit(u[0, pl.ds(r, 128), lanes]),
                limit(u[1, pl.ds(r, 128), lanes]),
            )
            msg = jnp.zeros((16, 128), f32)
            for k, x in enumerate(parts):
                msg = msg + lax.dot_general(
                    select(side, k), x.astype(bf16), (((1,), (1,)), ((), ())),
                    preferred_element_type=f32)
            outbox[side, :, dst] = msg.astype(bf16)
        return carry

    lax.fori_loop(0, 5, pack_edges, 0)

    pl.semaphore_wait(barrier, NROW + NCOL - 2)

    def col_copy(side):
        return pltpu.make_async_remote_copy(
            src_ref=outbox.at[side], dst_ref=inbox.at[side],
            send_sem=col_send.at[side], recv_sem=col_recv.at[side],
            device_id=(row, left if side == 0 else right), device_id_type=MESH)

    for side in range(2):
        col_copy(side).start()

    def row_copies(side):
        dev = (down if side == 0 else up, col)
        src_at = ROWS - HALO if side == 0 else 0
        dst_at = 0 if side == 0 else ROWS + HALO
        return (
            pltpu.make_async_remote_copy(
                src_ref=u_hbm.at[:, pl.ds(src_at, HALO), :], dst_ref=u.at[:, pl.ds(dst_at, HALO), :],
                send_sem=row_send.at[3 * side], recv_sem=row_recv.at[3 * side],
                device_id=dev, device_id_type=MESH),
            pltpu.make_async_remote_copy(
                src_ref=su_hbm.at[pl.ds(src_at, HALO), :], dst_ref=su.at[pl.ds(dst_at, HALO), :],
                send_sem=row_send.at[3 * side + 1], recv_sem=row_recv.at[3 * side + 1],
                device_id=dev, device_id_type=MESH),
        )

    def halo_tile_copy(side):
        dev = (down if side == 0 else up, col)
        src_at = ROWS if side == 0 else HALO
        dst_at = 0 if side == 0 else ROWS + HALO
        return pltpu.make_async_remote_copy(
            src_ref=ht.at[:, pl.ds(src_at, HALO), :], dst_ref=ht.at[:, pl.ds(dst_at, HALO), :],
            send_sem=row_send.at[3 * side + 2], recv_sem=row_recv.at[3 * side + 2],
            device_id=dev, device_id_type=MESH)

    for side in range(2):
        for cp in row_copies(side):
            cp.start()
    for j in (6, 2, 7, 1, 8, 0, 9):
        for cp in piece_copies(j):
            cp.start()

    def clear(o, carry):
        prod[o] = jnp.zeros((TILE, TILE), f32)
        return carry

    lax.fori_loop(0, 9, clear, 0)

    for side in range(2):
        col_copy(side).wait_recv()

    def unpack_edges(b, carry):
        r = pl.multiple_of(HALO + 128 * b, 8)
        src = pl.ds(pl.multiple_of(128 * b, 128), 128)
        for k in range(3):
            tile = jnp.zeros((128, 128), f32)
            for side in range(2):
                tile = tile + lax.dot_general(
                    inbox[side, :, src], select(side, k), (((0,), (0,)), ((), ())),
                    preferred_element_type=f32)
            ht[k, pl.ds(r, 128), :] = tile
        return carry

    lax.fori_loop(0, 5, unpack_edges, 0)
    for side in range(2):
        halo_tile_copy(side).start()

    def y_copy(c):
        return pltpu.make_async_remote_copy(
            src_ref=buf.at[c, pl.ds(own, 8)], dst_ref=buf.at[c, pl.ds(far, 8)],
            send_sem=ys.at[c], recv_sem=yr.at[c],
            device_id=(row, ycol), device_id_type=MESH)

    def x_copy(c):
        return pltpu.make_async_remote_copy(
            src_ref=buf.at[c, pl.ds(24, 8)], dst_ref=buf.at[c, pl.ds(8, 8)],
            send_sem=xs.at[c], recv_sem=xr.at[c],
            device_id=(row, xcol), device_id_type=MESH)

    def w_copy(j):
        at = pl.multiple_of(j * UNIT, UNIT)
        return pltpu.make_async_copy(
            wn.at[pl.ds(at, UNIT), :], w_hbm.at[pl.ds(at, UNIT), :], w_sem.at[j])

    sub = lax.broadcasted_iota(jnp.int32, (8, WIDE), 0)
    parity = lax.rem(sub + lax.broadcasted_iota(jnp.int32, (8, WIDE), 1), 2)

    for j in (4, 3):
        for cp in piece_copies(j)[:2]:
            cp.wait()

    def unit(k, carry):
        odd = lax.rem(k, 2)
        c = lax.div(k, 2)
        j = (4 - c) * (1 - odd) + (5 + c) * odd
        keep = 1 - lax.rem(k + par, 2)
        row0 = j * UNIT
        more = j + 2 * odd - 1 + 2 * jnp.maximum(1 - k, 0)

        @pl.when(k < 8)
        def _():
            for cp in piece_copies(more)[:2]:
                cp.wait()

        for side in range(2):
            @pl.when(k == 8 + side)
            def _():
                for cp in row_copies(side):
                    cp.wait_recv()
                halo_tile_copy(side).wait_recv()

        piece_copies(j)[2].wait()

        def fill(g, carry):
            r = pl.multiple_of(8 * g, 8)
            e = pl.multiple_of(row0 + 8 * g, 8)
            wk[pl.ds(r + 8, 8), 0:CB] = (2 * su[pl.ds(e, 8), :] - 1).astype(f32)
            wk[pl.ds(r + 8, 8), CB:WIDE] = ht[0, pl.ds(e, 8), :]
            return carry

        lax.fori_loop(0, 10, fill, 0)

        def half(h, carry):
            sweep = lax.div(h, 2)
            coloured = parity == lax.rem(h, 2)

            def group(g, carry):
                r = pl.multiple_of(8 * g, 8)
                e = pl.multiple_of(row0 + 8 * g, 8)
                before = wk[pl.ds(r, 8), :]
                cur = wk[pl.ds(r + 8, 8), :]
                after = wk[pl.ds(r + 16, 8), :]
                near = (
                    pltpu.roll(jnp.where(sub == 7, before, cur), 1, 0)
                    + pltpu.roll(jnp.where(sub == 0, after, cur), 7, 0)
                    + pltpu.roll(cur, 1, 1)
                    + pltpu.roll(cur, WIDE - 1, 1)
                )
                bound = jnp.concatenate(
                    [limit(u[sweep, pl.ds(e, 8), :]), ht[1 + sweep, pl.ds(e, 8), :]], axis=1)
                flip = coloured & (cur * near <= bound)
                wk[pl.ds(r + 8, 8), :] = jnp.where(flip, -cur, cur)
                return carry

            lax.fori_loop(0, 10, group, 0)
            return carry

        lax.fori_loop(0, 4, half, 0)

        base = own * keep + 24 * (1 - keep)

        def weigh(g, carry):
            r = pl.multiple_of(16 * g, 16)
            a = pl.multiple_of(row0 + 16 * g, 16)
            w = m[pl.ds(a, 16), :] * wk[pl.ds(r + 16, 16), 0:CB].astype(bf16)
            for t in range(8):
                buf[c, base + t, pl.ds(r, 16), :] = w[:, TILE * t:TILE * (t + 1)]
            wn[pl.ds(a, 16), :] = w
            return carry

        lax.fori_loop(0, 4, weigh, 0)

        @pl.when(keep == 1)
        def _():
            y_copy(c).start()

        @pl.when(keep == 0)
        def _():
            x_copy(c).start()

        w_copy(j).start()
        return carry

    lax.fori_loop(0, 10, unit, 0)

    def chunk(c, carry):
        y_copy(c).wait_recv()
        x_copy(c).wait_recv()
        for t in range(8):
            rows2 = buf[c, 2 * t:2 * t + 2].reshape(128, TILE)
            lt[:, 128 * t:128 * (t + 1)] = rows2.T

        def offset(o, carry):
            rhs = buf[c, pl.ds(o, 16)].reshape(16 * UNIT, TILE)
            prod[o] += jnp.dot(lt[...], rhs, preferred_element_type=f32)
            return carry

        lax.fori_loop(0, 9, offset, 0)
        return carry

    lax.fori_loop(0, CHUNKS, chunk, 0)

    def fold_128(b, carry):
        r = pl.multiple_of(8 * b, 8)
        lo = jnp.concatenate([prod[o, pl.ds(r, 8), :] for o in range(9)], axis=1)
        hi = jnp.concatenate([prod[o, pl.ds(r + 128, 8), :] for o in range(9)], axis=1)
        fold[pl.ds(r, 8), :] = lo[:, 0:WIDE] + hi[:, 128:128 + WIDE]
        return carry

    lax.fori_loop(0, 16, fold_128, 0)
    for n in (64, 32, 16, 8):
        def fold_n(b, carry, n=n):
            r = pl.multiple_of(8 * b, 8)
            fold[pl.ds(r, 8), :] += pltpu.roll(fold[pl.ds(r + n, 8), :], WIDE - n, 1)
            return carry

        lax.fori_loop(0, n // 8, fold_n, 0)
    v = fold[0:8, :]
    for n in (4, 2, 1):
        v = v + pltpu.roll(pltpu.roll(v, WIDE - n, 1), 8 - n, 0)

    for i in range(NROW):
        vb[i] = v[0:1, 128 * i:128 * (i + 1)]

    def r1_copy(i):
        to = lax.rem(row + i, NROW)
        return pltpu.make_async_remote_copy(
            src_ref=vb.at[to], dst_ref=rs1.at[i], send_sem=r1s.at[i], recv_sem=r1r.at[i],
            device_id=(to, col), device_id_type=MESH)

    for i in range(1, NROW):
        r1_copy(i).start()
    total = vb[row]
    for i in range(1, NROW):
        r1_copy(i).wait_recv()
        total = total + rs1[i]
    sb[...] = total

    def r2_copy(i):
        return pltpu.make_async_remote_copy(
            src_ref=sb, dst_ref=rs2.at[i], send_sem=r2s.at[i], recv_sem=r2r.at[i],
            device_id=(row, lax.rem(col + i, NCOL)), device_id_type=MESH)

    for i in range(1, NCOL):
        r2_copy(i).start()
    for i in range(1, NCOL):
        r2_copy(i).wait_recv()
        total = total + rs2[i]
    total = total * (1.0 / math.sqrt(ROWS * NROW * CB * NCOL))
    total = pltpu.roll(jnp.broadcast_to(total, (8, 128)), lax.rem(128 - 16 * col, 128), 1)
    corr_ref[...] = total

    for side in range(2):
        col_copy(side).wait_send()
        for cp in row_copies(side):
            cp.wait_send()
        halo_tile_copy(side).wait_send()

    def drain(c, carry):
        y_copy(c).wait_send()
        x_copy(c).wait_send()
        w_copy(2 * c).wait()
        w_copy(2 * c + 1).wait()
        return carry

    lax.fori_loop(0, CHUNKS, drain, 0)
    for i in range(1, NROW):
        r1_copy(i).wait_send()
    for i in range(1, NCOL):
        r2_copy(i).wait_send()


def on_device(spins_up, uniforms, moments, accept_bar):
    f32, bf16 = jnp.float32, jnp.bfloat16
    vmem, dma = pltpu.VMEM, pltpu.SemaphoreType.DMA
    hbm = pl.BlockSpec(memory_space=pl.ANY)
    weighted, corr = pl.pallas_call(
        kernel,
        out_shape=(
            jax.ShapeDtypeStruct((ROWS, CB), bf16),
            jax.ShapeDtypeStruct((8, 128), f32),
        ),
        in_specs=[hbm, hbm, hbm, pl.BlockSpec(memory_space=pltpu.SMEM)],
        out_specs=(hbm, pl.BlockSpec(memory_space=pltpu.VMEM)),
        scratch_shapes=[
            vmem((ROWS + 16, CB), jnp.int32),
            vmem((2, ROWS + 16, CB), f32),
            vmem((ROWS, CB), bf16),
            vmem((3, ROWS + 16, 128), f32),
            vmem((UNIT + 32, WIDE), f32),
            vmem((ROWS, CB), bf16),
            vmem((CHUNKS, 32, UNIT, TILE), bf16),
            vmem((TILE, 16 * UNIT), bf16),
            vmem((9, TILE, TILE), f32),
            vmem((128, WIDE), f32),
            vmem((2, 16, ROWS), bf16),
            vmem((2, 16, ROWS), bf16),
            vmem((NROW, 1, 128), f32),
            vmem((NROW, 1, 128), f32),
            vmem((NCOL, 1, 128), f32),
            vmem((1, 128), f32),
            dma((4,)), dma((10,)), dma((10,)), dma((10,)), dma((10,)),
            dma((2,)), dma((2,)), dma((6,)), dma((6,)),
            dma((CHUNKS,)), dma((CHUNKS,)), dma((CHUNKS,)), dma((CHUNKS,)),
            dma((NROW,)), dma((NROW,)), dma((NCOL,)), dma((NCOL,)),
        ],
        compiler_params=pltpu.CompilerParams(
            collective_id=0, has_side_effects=True, vmem_limit_bytes=56 * 1024 * 1024,
        ),
    )(spins_up, uniforms, moments, accept_bar)
    lattice = jnp.where(weighted > 0, 1.0, -1.0).astype(f32)
    return lattice, corr[0, :16]


def solution(mesh):
    placed = (P("row", "col"), P(None, "row", "col"), P("row", "col"), P())
    return jax.shard_map(
        on_device,
        mesh=mesh,
        in_specs=placed,
        out_specs=(P("row", "col"), P(("row", "col"))),
        check_vma=False,
    )
```

time: 360 us -> 96.8 us (0.27)
  Pallas kernels: 0 us -> 90.2 us
  other arithmetic: 71.7 us -> 4.6 us
  blocking collectives: 63.1 us -> 0 us
  local copies, waits for them, and re-layouts: 62 us -> 1.19 us
  matrix products: 57.3 us -> 0 us
  waiting for transfers between devices: 37.1 us -> 0 us
  starting transfers between devices: 32.7 us -> 0 us
  loops' own time: 32.1 us -> 0 us
    pallas_call x0 -> x1, Pallas kernels: none -> 90.2 us  [on_device(): pl.pallas_call(kernel, out_shape=(jax.ShapeDtypeStruct((ROWS, CB), bf16),...]
    unnamed x1 -> x0, blocking collectives: 63.1 us -> none
    dot_general x17 -> x0, matrix products: 57.3 us -> none  [product(): jnp.einsum('itp,itq->pq', left_tiles, shifted, preferred_element_type=jnp...]
    another operation x1 -> x0, loops' own time: 32.1 us -> none  [correlate(): products = lax.map(product, jnp.arange(offsets + 1, dtype=jnp.int32))]
    ppermute x12 -> x0, starting transfers between devices: 27.4 us -> none  [the longest x6 26 us: with_halo(): after = lax.ppermute(leading, axis, down)]
    all_to_all x1 -> x0, waiting for transfers between devices: 25.9 us -> none  [on_device(): lax.all_to_all(weighted, 'col', split_axis=0, concat_axis=1, tiled=True)]
    select_n x2 -> x1, other arithmetic: 30.1 us -> 4.6 us  [on_device(): lattice = jnp.where(weighted > 0, 1.0, -1.0).astype(f32)]
    concatenate x3 -> x0, local copies, waits for them, and re-layouts: 23.5 us -> none  [with_halo(): value = jnp.concatenate([before, value, after], axis=dim)]
  transfers between devices with their start and end apart: 13 -> 0, of which waited for: 6 -> 0; matrix products, arithmetic and copies ran while one was open for 6% -> 0% of each run, Pallas kernels for 0% -> 0%
where the time goes in v1:
time: 96.8 us; the launch traced here: 96.6 us
  Pallas kernels  90.2 us (93%)
  other arithmetic  4.6 us (5%)
  local copies, waits for them, and re-layouts  1.19 us (1%)
    pallas_call x1, Pallas kernels, on_device(): pl.pallas_call(kernel, out_shape=(jax.ShapeDtypeStruct((ROWS, CB), bf16),...  90.2 us
    select_n x1, other arithmetic, on_device(): lattice = jnp.where(weighted > 0, 1.0, -1.0).astype(f32)  4.6 us

profile of v1, /device:TPU:0, one launch (start us, length us, event | category | flops | bytes accessed | tf_op | source)
XLA Modules:
  0.0 96.6 jit_solution(12344704270872337659)
XLA Ops:
  0.6 90.2 %shard_map.59 = (bf16[640,2048]{1,0:T(8,128)(2,1)}, f32[8,128]{1,0:T(8,128)}) custom-call(s32[640,2048]{1,0:T(8,128)} %su_hbm.1, f32[2,640,2048]{2,1,0:T(8,128)} %u_hbm.1, bf16[640,2048]{1,0:T(8,128)(2,1)} %m_hbm.1, f32[2]{0:T(128)} %bar.1), custom_call_target="tpu_custom_call" | custom-call | tf_op jit(solution)/shard_map/pallas_call | solution.py:384
  90.8 1.2 %slice_bitcast_fusion = f32[16]{0:T(128)} fusion(f32[8,128]{1,0:T(8,128)} %get-tuple-element.5), kind=kLoop, calls=%fused_computation.1 | loop fusion | bytes 128 | tf_op jit(solution)/shard_map/squeeze | solution.py:419
  92.0 4.6 %compare_select_fusion = f32[640,2048]{1,0:T(8,128)} fusion(bf16[640,2048]{1,0:T(8,128)(2,1)} %get-tuple-element.4), kind=kLoop, calls=%fused_computation | loop fusion | flops 2621440 | bytes 7864320 | tf_op jit(solution)/shard_map/jit(_where)/select_n | solution.py:418

commit v2 on v1

--- a/solution.py
+++ b/solution.py
@@ -17,13 +17,18 @@
 CHUNKS = 5
 WIDE = CB + 128
 TILE = 256
+LT = CB // 128
+EDGES = (0, LT - 1)
+BANDS = ((184, 272), (0, 184), (456, 184), (0, 640))
+SPAN = (UNIT + 2 * HALO) // 8
+PAIRS = SPAN // 2
 MESH = pl.DeviceIdType.MESH
 
 
 def kernel(
     su_hbm, u_hbm, m_hbm, bar, w_hbm, corr_ref,
-    su, u, m, ht, wk, wn, buf, lt, prod, fold, outbox, inbox, vb, rs1, rs2, sb,
-    edge_sem, u_sem, s_sem, m_sem, w_sem, col_send, col_recv,
+    su, u, hu, hs, m, ht, c0, c1, wk, wn, buf, lt, prod, fold, outbox, inbox, vb, rs1, rs2, sb,
+    u_sem, s_sem, m_sem, w_sem, col_send, col_recv,
     row_send, row_recv, ys, yr, xs, xr, r1s, r1r, r2s, r2r,
 ):
     f32, bf16 = jnp.float32, jnp.bfloat16
@@ -47,35 +52,37 @@
             barrier, inc=1, device_id=(row, lax.rem(col + i, NCOL)), device_id_type=MESH
         )
 
-    def edge_copies():
-        out = []
-        for e, lo in enumerate((0, CB - 128)):
-            lanes = pl.ds(lo, 128)
-            out.append(pltpu.make_async_copy(
-                u_hbm.at[:, :, lanes], u.at[:, pl.ds(HALO, ROWS), lanes], edge_sem.at[2 * e]))
-            out.append(pltpu.make_async_copy(
-                su_hbm.at[:, lanes], su.at[pl.ds(HALO, ROWS), lanes], edge_sem.at[2 * e + 1]))
-        return out
-
-    inner = pl.ds(128, CB - 256)
-
-    def piece_copies(j):
-        at = pl.multiple_of(j * UNIT, UNIT)
-        to = pl.multiple_of(j * UNIT + HALO, 8)
+    def tile_copies(t, band):
+        at, size = BANDS[band]
+        lanes = pl.ds(128 * t, 128)
         return (
             pltpu.make_async_copy(
-                u_hbm.at[:, pl.ds(at, UNIT), inner], u.at[:, pl.ds(to, UNIT), inner], u_sem.at[j]),
+                u_hbm.at[:, pl.ds(at, size), lanes],
+                u.at[:, t, pl.ds(at + HALO, size), :], u_sem.at[band, t]),
             pltpu.make_async_copy(
-                su_hbm.at[pl.ds(at, UNIT), inner], su.at[pl.ds(to, UNIT), inner], s_sem.at[j]),
-            pltpu.make_async_copy(
-                m_hbm.at[pl.ds(at, UNIT), :], m.at[pl.ds(at, UNIT), :], m_sem.at[j]),
+                su_hbm.at[pl.ds(at, size), lanes],
+                su.at[t, pl.ds(at + HALO, size), :], s_sem.at[band, t]),
         )
 
-    for cp in edge_copies():
-        cp.start()
-    for j in (4, 3, 5):
-        for cp in piece_copies(j):
-            cp.start()
+    def m_copy(j):
+        at = pl.multiple_of(j * UNIT, UNIT)
+        return pltpu.make_async_copy(
+            m_hbm.at[pl.ds(at, UNIT), :], m.at[pl.ds(at, UNIT), :], m_sem.at[j])
+
+    def start_band(band):
+        tiles = EDGES if band == 3 else range(1, LT - 1)
+        for t in tiles:
+            for cp in tile_copies(t, band):
+                cp.start()
+
+    def wait_band(band):
+        tiles = EDGES if band == 3 else range(1, LT - 1)
+        for t in tiles:
+            for cp in tile_copies(t, band):
+                cp.wait()
+
+    start_band(3)
+    start_band(0)
 
     a0 = bar[0]
     a1 = bar[1]
@@ -90,20 +97,17 @@
         hit = (c >= 0) & (c < 4) & (r == 4 * k + c)
         return jnp.where(hit, 1.0, 0.0).astype(bf16)
 
-    wk[0:8, :] = jnp.zeros((8, WIDE), f32)
-    wk[88:96, :] = jnp.zeros((8, WIDE), f32)
-    for cp in edge_copies():
-        cp.wait()
+    wait_band(3)
 
     def pack_edges(b, carry):
         r = pl.multiple_of(HALO + 128 * b, 8)
         dst = pl.ds(pl.multiple_of(128 * b, 128), 128)
         for side in range(2):
-            lanes = pl.ds(side * (CB - 128), 128)
+            t = EDGES[side]
             parts = (
-                (2 * su[pl.ds(r, 128), lanes] - 1).astype(f32),
-                limit(u[0, pl.ds(r, 128), lanes]),
-                limit(u[1, pl.ds(r, 128), lanes]),
+                (2 * su[t, pl.ds(r, 128), :] - 1).astype(f32),
+                limit(u[0, t, pl.ds(r, 128), :]),
+                limit(u[1, t, pl.ds(r, 128), :]),
             )
             msg = jnp.zeros((16, 128), f32)
             for k, x in enumerate(parts):
@@ -129,14 +133,13 @@
     def row_copies(side):
         dev = (down if side == 0 else up, col)
         src_at = ROWS - HALO if side == 0 else 0
-        dst_at = 0 if side == 0 else ROWS + HALO
         return (
             pltpu.make_async_remote_copy(
-                src_ref=u_hbm.at[:, pl.ds(src_at, HALO), :], dst_ref=u.at[:, pl.ds(dst_at, HALO), :],
+                src_ref=u_hbm.at[:, pl.ds(src_at, HALO), :], dst_ref=hu.at[side],
                 send_sem=row_send.at[3 * side], recv_sem=row_recv.at[3 * side],
                 device_id=dev, device_id_type=MESH),
             pltpu.make_async_remote_copy(
-                src_ref=su_hbm.at[pl.ds(src_at, HALO), :], dst_ref=su.at[pl.ds(dst_at, HALO), :],
+                src_ref=su_hbm.at[pl.ds(src_at, HALO), :], dst_ref=hs.at[side],
                 send_sem=row_send.at[3 * side + 1], recv_sem=row_recv.at[3 * side + 1],
                 device_id=dev, device_id_type=MESH),
         )
@@ -153,9 +156,12 @@
     for side in range(2):
         for cp in row_copies(side):
             cp.start()
-    for j in (6, 2, 7, 1, 8, 0, 9):
-        for cp in piece_copies(j):
-            cp.start()
+    for j in (4, 5, 3, 6):
+        m_copy(j).start()
+    for band in (1, 2):
+        start_band(band)
+    for j in (2, 7, 1, 8, 0, 9):
+        m_copy(j).start()
 
     def clear(o, carry):
         prod[o] = jnp.zeros((TILE, TILE), f32)
@@ -199,12 +205,17 @@
         return pltpu.make_async_copy(
             wn.at[pl.ds(at, UNIT), :], w_hbm.at[pl.ds(at, UNIT), :], w_sem.at[j])
 
-    sub = lax.broadcasted_iota(jnp.int32, (8, WIDE), 0)
-    parity = lax.rem(sub + lax.broadcasted_iota(jnp.int32, (8, WIDE), 1), 2)
-
-    for j in (4, 3):
-        for cp in piece_copies(j)[:2]:
-            cp.wait()
+    lane = lax.broadcasted_iota(jnp.int32, (8, 128), 1)
+    even = lax.rem(lane, 2) == 0
+    first, last = lane == 0, lane == 127
+    colours = (c0, c1)
+
+    def wrap(ref):
+        for t in range(LT + 1):
+            ref[0, t] = pltpu.roll(ref[PAIRS, t], 1, 0)
+            ref[PAIRS + 1, t] = pltpu.roll(ref[1, t], 7, 0)
+
+    wait_band(0)
 
     def unit(k, carry):
         odd = lax.rem(k, 2)
@@ -212,67 +223,88 @@
         j = (4 - c) * (1 - odd) + (5 + c) * odd
         keep = 1 - lax.rem(k + par, 2)
         row0 = j * UNIT
-        more = j + 2 * odd - 1 + 2 * jnp.maximum(1 - k, 0)
-
-        @pl.when(k < 8)
-        def _():
-            for cp in piece_copies(more)[:2]:
-                cp.wait()
 
         for side in range(2):
+            @pl.when(k == 4 + side)
+            def _():
+                wait_band(1 + side)
+
             @pl.when(k == 8 + side)
             def _():
                 for cp in row_copies(side):
                     cp.wait_recv()
                 halo_tile_copy(side).wait_recv()
-
-        piece_copies(j)[2].wait()
+                at = 0 if side == 0 else ROWS + HALO
+                for t in range(LT):
+                    lanes = pl.ds(128 * t, 128)
+                    su[t, at:at + HALO, :] = hs[side, :, lanes]
+                    for n in range(2):
+                        u[n, t, at:at + HALO, :] = hu[side, n, :, lanes]
+
+        m_copy(j).wait()
 
         def fill(g, carry):
-            r = pl.multiple_of(8 * g, 8)
-            e = pl.multiple_of(row0 + 8 * g, 8)
-            wk[pl.ds(r + 8, 8), 0:CB] = (2 * su[pl.ds(e, 8), :] - 1).astype(f32)
-            wk[pl.ds(r + 8, 8), CB:WIDE] = ht[0, pl.ds(e, 8), :]
+            upper = pl.ds(row0 + 2 * g, 8, stride=SPAN)
+            lower = pl.ds(row0 + 2 * g + 1, 8, stride=SPAN)
+            for t in range(LT + 1):
+                if t < LT:
+                    a = (2 * su[t, upper, :] - 1).astype(f32)
+                    b = (2 * su[t, lower, :] - 1).astype(f32)
+                else:
+                    a, b = ht[0, upper, :], ht[0, lower, :]
+                c0[g + 1, t] = jnp.where(even, a, b)
+                c1[g + 1, t] = jnp.where(even, b, a)
             return carry
 
-        lax.fori_loop(0, 10, fill, 0)
-
-        def half(h, carry):
-            sweep = lax.div(h, 2)
-            coloured = parity == lax.rem(h, 2)
+        lax.fori_loop(0, PAIRS, fill, 0)
+        wrap(c1)
+
+        for h in range(4):
+            sweep, colour = h // 2, h % 2
+            mine, other = colours[colour], colours[1 - colour]
 
             def group(g, carry):
-                r = pl.multiple_of(8 * g, 8)
-                e = pl.multiple_of(row0 + 8 * g, 8)
-                before = wk[pl.ds(r, 8), :]
-                cur = wk[pl.ds(r + 8, 8), :]
-                after = wk[pl.ds(r + 16, 8), :]
-                near = (
-                    pltpu.roll(jnp.where(sub == 7, before, cur), 1, 0)
-                    + pltpu.roll(jnp.where(sub == 0, after, cur), 7, 0)
-                    + pltpu.roll(cur, 1, 1)
-                    + pltpu.roll(cur, WIDE - 1, 1)
-                )
-                bound = jnp.concatenate(
-                    [limit(u[sweep, pl.ds(e, 8), :]), ht[1 + sweep, pl.ds(e, 8), :]], axis=1)
-                flip = coloured & (cur * near <= bound)
-                wk[pl.ds(r + 8, 8), :] = jnp.where(flip, -cur, cur)
+                upper = pl.ds(row0 + 2 * g + colour, 8, stride=SPAN)
+                lower = pl.ds(row0 + 2 * g + 1 - colour, 8, stride=SPAN)
+                mid = [other[g + 1, t] for t in range(LT + 1)]
+                east = [pltpu.roll(x, 1, 1) for x in mid]
+                west = [pltpu.roll(x, 127, 1) for x in mid]
+                for t in range(LT + 1):
+                    above, below = other[g, t], other[g + 2, t]
+                    outer = jnp.where(even, above, below) if colour == 0 else jnp.where(even, below, above)
+                    side = (jnp.where(first, east[t - 1], east[t])
+                            + jnp.where(last, west[(t + 1) % (LT + 1)], west[t]))
+                    if t < LT:
+                        bound = limit(jnp.where(even, u[sweep, t, upper, :], u[sweep, t, lower, :]))
+                    else:
+                        bound = jnp.where(even, ht[1 + sweep, upper, :], ht[1 + sweep, lower, :])
+                    cur = mine[g + 1, t]
+                    flip = cur * (mid[t] + outer + side) <= bound
+                    mine[g + 1, t] = jnp.where(flip, -cur, cur)
                 return carry
 
-            lax.fori_loop(0, 10, group, 0)
+            lax.fori_loop(0, PAIRS, group, 0)
+            if h < 3:
+                wrap(mine)
+
+        def spread(g, carry):
+            for t in range(LT):
+                a, b = c0[g + 1, t], c1[g + 1, t]
+                wk[t, pl.ds(2 * g, 8, stride=SPAN), :] = jnp.where(even, a, b)
+                wk[t, pl.ds(2 * g + 1, 8, stride=SPAN), :] = jnp.where(even, b, a)
             return carry
 
-        lax.fori_loop(0, 4, half, 0)
-
+        lax.fori_loop(0, PAIRS, spread, 0)
         base = own * keep + 24 * (1 - keep)
 
         def weigh(g, carry):
             r = pl.multiple_of(16 * g, 16)
             a = pl.multiple_of(row0 + 16 * g, 16)
-            w = m[pl.ds(a, 16), :] * wk[pl.ds(r + 16, 16), 0:CB].astype(bf16)
-            for t in range(8):
-                buf[c, base + t, pl.ds(r, 16), :] = w[:, TILE * t:TILE * (t + 1)]
-            wn[pl.ds(a, 16), :] = w
+            for t in range(LT):
+                lanes = pl.ds(128 * t, 128)
+                w = m[pl.ds(a, 16), lanes] * wk[t, pl.ds(r + 8, 16), :].astype(bf16)
+                buf[c, base + t // 2, pl.ds(r, 16), 128 * (t % 2):128 * (t % 2 + 1)] = w
+                wn[pl.ds(a, 16), lanes] = w
             return carry
 
         lax.fori_loop(0, 4, weigh, 0)
@@ -390,11 +422,15 @@
         in_specs=[hbm, hbm, hbm, pl.BlockSpec(memory_space=pltpu.SMEM)],
         out_specs=(hbm, pl.BlockSpec(memory_space=pltpu.VMEM)),
         scratch_shapes=[
-            vmem((ROWS + 16, CB), jnp.int32),
-            vmem((2, ROWS + 16, CB), f32),
+            vmem((LT, ROWS + 16, 128), jnp.int32),
+            vmem((2, LT, ROWS + 16, 128), f32),
+            vmem((2, 2, HALO, CB), f32),
+            vmem((2, HALO, CB), jnp.int32),
             vmem((ROWS, CB), bf16),
             vmem((3, ROWS + 16, 128), f32),
-            vmem((UNIT + 32, WIDE), f32),
+            vmem((PAIRS + 2, LT + 1, 8, 128), f32),
+            vmem((PAIRS + 2, LT + 1, 8, 128), f32),
+            vmem((LT, UNIT + 16, 128), f32),
             vmem((ROWS, CB), bf16),
             vmem((CHUNKS, 32, UNIT, TILE), bf16),
             vmem((TILE, 16 * UNIT), bf16),
@@ -406,7 +442,7 @@
             vmem((NROW, 1, 128), f32),
             vmem((NCOL, 1, 128), f32),
             vmem((1, 128), f32),
-            dma((4,)), dma((10,)), dma((10,)), dma((10,)), dma((10,)),
+            dma((4, LT)), dma((4, LT)), dma((10,)), dma((10,)),
             dma((2,)), dma((2,)), dma((6,)), dma((6,)),
             dma((CHUNKS,)), dma((CHUNKS,)), dma((CHUNKS,)), dma((CHUNKS,)),
             dma((NROW,)), dma((NROW,)), dma((NCOL,)), dma((NCOL,)),

time: 96.8 us -> 73.7 us (0.76)
  Pallas kernels: 90.2 us -> 67.1 us
    pallas_call x1, Pallas kernels: 90.2 us -> 67.1 us  [on_device(): pl.pallas_call(kernel, out_shape=(jax.ShapeDtypeStruct((ROWS, CB), bf16),...]
where the time goes in v2:
time: 73.7 us; the launch traced here: 73.5 us
  Pallas kernels  67.1 us (91%)
  other arithmetic  4.6 us (6%)
  local copies, waits for them, and re-layouts  1.19 us (2%)
    pallas_call x1, Pallas kernels, on_device(): pl.pallas_call(kernel, out_shape=(jax.ShapeDtypeStruct((ROWS, CB), bf16),...  67.1 us
    select_n x1, other arithmetic, on_device(): lattice = jnp.where(weighted > 0, 1.0, -1.0).astype(f32)  4.6 us

profile of v2, /device:TPU:0, one launch (start us, length us, event | category | flops | bytes accessed | tf_op | source)
XLA Modules:
  0.0 73.5 jit_solution(2179618695030246938)
XLA Ops:
  0.6 67.1 %shard_map.59 = (bf16[640,2048]{1,0:T(8,128)(2,1)}, f32[8,128]{1,0:T(8,128)}) custom-call(s32[640,2048]{1,0:T(8,128)} %su_hbm.1, f32[2,640,2048]{2,1,0:T(8,128)} %u_hbm.1, bf16[640,2048]{1,0:T(8,128)(2,1)} %m_hbm.1, f32[2]{0:T(128)} %bar.1), custom_call_target="tpu_custom_call" | custom-call | tf_op jit(solution)/shard_map/pallas_call | solution.py:416
  67.7 1.2 %slice_bitcast_fusion = f32[16]{0:T(128)} fusion(f32[8,128]{1,0:T(8,128)} %get-tuple-element.5), kind=kLoop, calls=%fused_computation.1 | loop fusion | bytes 128 | tf_op jit(solution)/shard_map/squeeze | solution.py:455
  68.9 4.6 %compare_select_fusion = f32[640,2048]{1,0:T(8,128)} fusion(bf16[640,2048]{1,0:T(8,128)(2,1)} %get-tuple-element.4), kind=kLoop, calls=%fused_computation | loop fusion | flops 2621440 | bytes 7864320 | tf_op jit(solution)/shard_map/jit(_where)/select_n | solution.py:454

commit v3 on v2

--- a/solution.py
+++ b/solution.py
@@ -14,21 +14,22 @@
 NCOL = 8
 HALO = 8
 UNIT = 64
-CHUNKS = 5
 WIDE = CB + 128
 TILE = 256
 LT = CB // 128
 EDGES = (0, LT - 1)
-BANDS = ((184, 272), (0, 184), (456, 184), (0, 640))
+BANDS = ((280, 80), (152, 128), (360, 128), (0, 152), (488, 152), (0, 640))
+M_BANDS = ((288, 64), (0, 288), (352, 288))
+PARTS = (32, 64, 64, 64, 64, 32)
 SPAN = (UNIT + 2 * HALO) // 8
 PAIRS = SPAN // 2
 MESH = pl.DeviceIdType.MESH
 
 
 def kernel(
-    su_hbm, u_hbm, m_hbm, bar, w_hbm, corr_ref,
-    su, u, hu, hs, m, ht, c0, c1, wk, wn, buf, lt, prod, fold, outbox, inbox, vb, rs1, rs2, sb,
-    u_sem, s_sem, m_sem, w_sem, col_send, col_recv,
+    su_hbm, u_hbm, m_hbm, bar, w_ref, corr_ref,
+    su, u, hu, hs, m, ht, c0, c1, wk, small, large, lt, prod, fold, outbox, inbox, vb, rs1, rs2, sb,
+    u_sem, s_sem, m_sem, col_send, col_recv,
     row_send, row_recv, ys, yr, xs, xr, r1s, r1r, r2s, r2r,
 ):
     f32, bf16 = jnp.float32, jnp.bfloat16
@@ -64,25 +65,25 @@
                 su.at[t, pl.ds(at + HALO, size), :], s_sem.at[band, t]),
         )
 
-    def m_copy(j):
-        at = pl.multiple_of(j * UNIT, UNIT)
-        return pltpu.make_async_copy(
-            m_hbm.at[pl.ds(at, UNIT), :], m.at[pl.ds(at, UNIT), :], m_sem.at[j])
+    def m_copy(band):
+        rows = pl.ds(*M_BANDS[band])
+        return pltpu.make_async_copy(m_hbm.at[rows, :], m.at[rows, :], m_sem.at[band])
 
     def start_band(band):
-        tiles = EDGES if band == 3 else range(1, LT - 1)
+        tiles = EDGES if band == 5 else range(1, LT - 1)
         for t in tiles:
             for cp in tile_copies(t, band):
                 cp.start()
 
     def wait_band(band):
-        tiles = EDGES if band == 3 else range(1, LT - 1)
+        tiles = EDGES if band == 5 else range(1, LT - 1)
         for t in tiles:
             for cp in tile_copies(t, band):
                 cp.wait()
 
-    start_band(3)
+    start_band(5)
     start_band(0)
+    m_copy(0).start()
 
     a0 = bar[0]
     a1 = bar[1]
@@ -97,11 +98,11 @@
         hit = (c >= 0) & (c < 4) & (r == 4 * k + c)
         return jnp.where(hit, 1.0, 0.0).astype(bf16)
 
-    wait_band(3)
-
-    def pack_edges(b, carry):
-        r = pl.multiple_of(HALO + 128 * b, 8)
-        dst = pl.ds(pl.multiple_of(128 * b, 128), 128)
+    wait_band(5)
+
+    for b in range(5):
+        r = HALO + 128 * b
+        dst = pl.ds(128 * b, 128)
         for side in range(2):
             t = EDGES[side]
             parts = (
@@ -115,9 +116,6 @@
                     select(side, k), x.astype(bf16), (((1,), (1,)), ((), ())),
                     preferred_element_type=f32)
             outbox[side, :, dst] = msg.astype(bf16)
-        return carry
-
-    lax.fori_loop(0, 5, pack_edges, 0)
 
     pl.semaphore_wait(barrier, NROW + NCOL - 2)
 
@@ -156,25 +154,18 @@
     for side in range(2):
         for cp in row_copies(side):
             cp.start()
-    for j in (4, 5, 3, 6):
-        m_copy(j).start()
     for band in (1, 2):
         start_band(band)
-    for j in (2, 7, 1, 8, 0, 9):
-        m_copy(j).start()
-
-    def clear(o, carry):
-        prod[o] = jnp.zeros((TILE, TILE), f32)
-        return carry
-
-    lax.fori_loop(0, 9, clear, 0)
+        m_copy(band).start()
+    for band in (3, 4):
+        start_band(band)
 
     for side in range(2):
         col_copy(side).wait_recv()
 
-    def unpack_edges(b, carry):
-        r = pl.multiple_of(HALO + 128 * b, 8)
-        src = pl.ds(pl.multiple_of(128 * b, 128), 128)
+    for b in range(5):
+        r = HALO + 128 * b
+        src = pl.ds(128 * b, 128)
         for k in range(3):
             tile = jnp.zeros((128, 128), f32)
             for side in range(2):
@@ -182,28 +173,23 @@
                     inbox[side, :, src], select(side, k), (((0,), (0,)), ((), ())),
                     preferred_element_type=f32)
             ht[k, pl.ds(r, 128), :] = tile
-        return carry
-
-    lax.fori_loop(0, 5, unpack_edges, 0)
     for side in range(2):
         halo_tile_copy(side).start()
 
-    def y_copy(c):
-        return pltpu.make_async_remote_copy(
-            src_ref=buf.at[c, pl.ds(own, 8)], dst_ref=buf.at[c, pl.ds(far, 8)],
+    def part(c):
+        return small.at[c // 5] if c in (0, 5) else large.at[c - 1]
+
+    def y_copy(c, ref):
+        return pltpu.make_async_remote_copy(
+            src_ref=ref.at[pl.ds(own, 8)], dst_ref=ref.at[pl.ds(far, 8)],
             send_sem=ys.at[c], recv_sem=yr.at[c],
             device_id=(row, ycol), device_id_type=MESH)
 
-    def x_copy(c):
-        return pltpu.make_async_remote_copy(
-            src_ref=buf.at[c, pl.ds(24, 8)], dst_ref=buf.at[c, pl.ds(8, 8)],
+    def x_copy(c, ref):
+        return pltpu.make_async_remote_copy(
+            src_ref=ref.at[pl.ds(24, 8)], dst_ref=ref.at[pl.ds(8, 8)],
             send_sem=xs.at[c], recv_sem=xr.at[c],
             device_id=(row, xcol), device_id_type=MESH)
-
-    def w_copy(j):
-        at = pl.multiple_of(j * UNIT, UNIT)
-        return pltpu.make_async_copy(
-            wn.at[pl.ds(at, UNIT), :], w_hbm.at[pl.ds(at, UNIT), :], w_sem.at[j])
 
     lane = lax.broadcasted_iota(jnp.int32, (8, 128), 1)
     even = lax.rem(lane, 2) == 0
@@ -215,21 +201,39 @@
             ref[0, t] = pltpu.roll(ref[PAIRS, t], 1, 0)
             ref[PAIRS + 1, t] = pltpu.roll(ref[1, t], 7, 0)
 
-    wait_band(0)
+    def weigh(c, ref, half, row0, start, count):
+        keep = 1 - lax.rem(half + par, 2)
+        base = own * keep + 24 * (1 - keep)
+        for g in range(count // 16):
+            at = pl.multiple_of(row0 + start + 16 * g, 16)
+            for t in range(LT):
+                lanes = pl.ds(128 * t, 128)
+                w = m[pl.ds(at, 16), lanes] * wk[t, HALO + start + 16 * g:HALO + start + 16 * g + 16, :].astype(bf16)
+                ref[base + t // 2, 16 * g:16 * g + 16, 128 * (t % 2):128 * (t % 2 + 1)] = w
+                w_ref[pl.ds(at, 16), lanes] = w
+
+        @pl.when(keep == 1)
+        def _():
+            y_copy(c, ref).start()
+
+        @pl.when(keep == 0)
+        def _():
+            x_copy(c, ref).start()
 
     def unit(k, carry):
+        i = lax.div(k + 1, 2)
         odd = lax.rem(k, 2)
-        c = lax.div(k, 2)
-        j = (4 - c) * (1 - odd) + (5 + c) * odd
-        keep = 1 - lax.rem(k + par, 2)
-        row0 = j * UNIT
+        row0 = jnp.minimum(jnp.maximum(288 + UNIT * i * (1 - 2 * odd), 0), ROWS - UNIT)
+
+        for n in range(4):
+            @pl.when(k == 1 + n)
+            def _():
+                wait_band(1 + n)
+                if n < 2:
+                    m_copy(1 + n).wait()
 
         for side in range(2):
-            @pl.when(k == 4 + side)
-            def _():
-                wait_band(1 + side)
-
-            @pl.when(k == 8 + side)
+            @pl.when(k == 9 + side)
             def _():
                 for cp in row_copies(side):
                     cp.wait_recv()
@@ -241,9 +245,7 @@
                     for n in range(2):
                         u[n, t, at:at + HALO, :] = hu[side, n, :, lanes]
 
-        m_copy(j).wait()
-
-        def fill(g, carry):
+        for g in range(PAIRS):
             upper = pl.ds(row0 + 2 * g, 8, stride=SPAN)
             lower = pl.ds(row0 + 2 * g + 1, 8, stride=SPAN)
             for t in range(LT + 1):
@@ -254,16 +256,13 @@
                     a, b = ht[0, upper, :], ht[0, lower, :]
                 c0[g + 1, t] = jnp.where(even, a, b)
                 c1[g + 1, t] = jnp.where(even, b, a)
-            return carry
-
-        lax.fori_loop(0, PAIRS, fill, 0)
         wrap(c1)
 
         for h in range(4):
             sweep, colour = h // 2, h % 2
             mine, other = colours[colour], colours[1 - colour]
 
-            def group(g, carry):
+            for g in range(PAIRS):
                 upper = pl.ds(row0 + 2 * g + colour, 8, stride=SPAN)
                 lower = pl.ds(row0 + 2 * g + 1 - colour, 8, stride=SPAN)
                 mid = [other[g + 1, t] for t in range(LT + 1)]
@@ -281,79 +280,66 @@
                     cur = mine[g + 1, t]
                     flip = cur * (mid[t] + outer + side) <= bound
                     mine[g + 1, t] = jnp.where(flip, -cur, cur)
-                return carry
-
-            lax.fori_loop(0, PAIRS, group, 0)
             if h < 3:
                 wrap(mine)
 
-        def spread(g, carry):
+        for g in range(PAIRS):
             for t in range(LT):
                 a, b = c0[g + 1, t], c1[g + 1, t]
                 wk[t, pl.ds(2 * g, 8, stride=SPAN), :] = jnp.where(even, a, b)
                 wk[t, pl.ds(2 * g + 1, 8, stride=SPAN), :] = jnp.where(even, b, a)
-            return carry
-
-        lax.fori_loop(0, PAIRS, spread, 0)
-        base = own * keep + 24 * (1 - keep)
-
-        def weigh(g, carry):
-            r = pl.multiple_of(16 * g, 16)
-            a = pl.multiple_of(row0 + 16 * g, 16)
-            for t in range(LT):
-                lanes = pl.ds(128 * t, 128)
-                w = m[pl.ds(a, 16), lanes] * wk[t, pl.ds(r + 8, 16), :].astype(bf16)
-                buf[c, base + t // 2, pl.ds(r, 16), 128 * (t % 2):128 * (t % 2 + 1)] = w
-                wn[pl.ds(a, 16), lanes] = w
-            return carry
-
-        lax.fori_loop(0, 4, weigh, 0)
-
-        @pl.when(keep == 1)
+
+        @pl.when(k == 0)
         def _():
-            y_copy(c).start()
-
-        @pl.when(keep == 0)
+            for half in range(2):
+                weigh(0, small.at[0], half, row0, 32 * half, 32)
+
+        @pl.when((k > 0) & (k < 9))
         def _():
-            x_copy(c).start()
-
-        w_copy(j).start()
+            weigh(i, large.at[i - 1], 1 - odd, row0, 0, UNIT)
+
+        for half in range(2):
+            @pl.when(k == 9 + half)
+            def _():
+                weigh(5, small.at[1], half, row0, 32 * half, 32)
+
         return carry
 
-    lax.fori_loop(0, 10, unit, 0)
-
-    def chunk(c, carry):
-        y_copy(c).wait_recv()
-        x_copy(c).wait_recv()
-        for t in range(8):
-            rows2 = buf[c, 2 * t:2 * t + 2].reshape(128, TILE)
-            lt[:, 128 * t:128 * (t + 1)] = rows2.T
-
-        def offset(o, carry):
-            rhs = buf[c, pl.ds(o, 16)].reshape(16 * UNIT, TILE)
-            prod[o] += jnp.dot(lt[...], rhs, preferred_element_type=f32)
-            return carry
-
-        lax.fori_loop(0, 9, offset, 0)
+    wait_band(0)
+    m_copy(0).wait()
+    lax.fori_loop(0, 11, unit, 0)
+
+    def chunk(c, ref, height, opening):
+        y_copy(c, ref).wait_recv()
+        x_copy(c, ref).wait_recv()
+        depth = 16 * height
+        per = 128 // height
+        for n in range(depth // 128):
+            rows = ref[per * n:per * n + per].reshape(128, TILE)
+            lt[:, 128 * n:128 * (n + 1)] = rows.T
+        for o in range(9):
+            right = ref[o:o + 16].reshape(depth, TILE)
+            p = jnp.dot(lt[:, 0:depth], right, preferred_element_type=f32)
+            prod[o] = p if opening else prod[o] + p
+
+    chunk(0, small.at[0], 32, True)
+
+    def middle(c, carry):
+        chunk(c + 1, large.at[c], UNIT, False)
         return carry
 
-    lax.fori_loop(0, CHUNKS, chunk, 0)
-
-    def fold_128(b, carry):
-        r = pl.multiple_of(8 * b, 8)
+    lax.fori_loop(0, 4, middle, 0)
+    chunk(5, small.at[1], 32, False)
+
+    for b in range(16):
+        r = 8 * b
         lo = jnp.concatenate([prod[o, pl.ds(r, 8), :] for o in range(9)], axis=1)
         hi = jnp.concatenate([prod[o, pl.ds(r + 128, 8), :] for o in range(9)], axis=1)
         fold[pl.ds(r, 8), :] = lo[:, 0:WIDE] + hi[:, 128:128 + WIDE]
-        return carry
-
-    lax.fori_loop(0, 16, fold_128, 0)
     for n in (64, 32, 16, 8):
-        def fold_n(b, carry, n=n):
-            r = pl.multiple_of(8 * b, 8)
+        for b in range(n // 8):
+            r = 8 * b
             fold[pl.ds(r, 8), :] += pltpu.roll(fold[pl.ds(r + n, 8), :], WIDE - n, 1)
-            return carry
-
-        lax.fori_loop(0, n // 8, fold_n, 0)
     v = fold[0:8, :]
     for n in (4, 2, 1):
         v = v + pltpu.roll(pltpu.roll(v, WIDE - n, 1), 8 - n, 0)
@@ -395,18 +381,18 @@
             cp.wait_send()
         halo_tile_copy(side).wait_send()
 
-    def drain(c, carry):
-        y_copy(c).wait_send()
-        x_copy(c).wait_send()
-        w_copy(2 * c).wait()
-        w_copy(2 * c + 1).wait()
-        return carry
-
-    lax.fori_loop(0, CHUNKS, drain, 0)
+    for c in range(len(PARTS)):
+        y_copy(c, part(c)).wait_send()
+        x_copy(c, part(c)).wait_send()
     for i in range(1, NROW):
         r1_copy(i).wait_send()
     for i in range(1, NCOL):
         r2_copy(i).wait_send()
+
+
+def finish(w_ref, reduced_ref, spins_ref, corr_ref):
+    spins_ref[...] = jnp.where(w_ref[...].astype(jnp.float32) > 0, 1.0, -1.0)
+    corr_ref[...] = reduced_ref[0, :16]
 
 
 def on_device(spins_up, uniforms, moments, accept_bar):
@@ -420,7 +406,7 @@
             jax.ShapeDtypeStruct((8, 128), f32),
         ),
         in_specs=[hbm, hbm, hbm, pl.BlockSpec(memory_space=pltpu.SMEM)],
-        out_specs=(hbm, pl.BlockSpec(memory_space=pltpu.VMEM)),
+        out_specs=(pl.BlockSpec(memory_space=pltpu.VMEM), pl.BlockSpec(memory_space=pltpu.VMEM)),
         scratch_shapes=[
             vmem((LT, ROWS + 16, 128), jnp.int32),
             vmem((2, LT, ROWS + 16, 128), f32),
@@ -431,8 +417,8 @@
             vmem((PAIRS + 2, LT + 1, 8, 128), f32),
             vmem((PAIRS + 2, LT + 1, 8, 128), f32),
             vmem((LT, UNIT + 16, 128), f32),
-            vmem((ROWS, CB), bf16),
-            vmem((CHUNKS, 32, UNIT, TILE), bf16),
+            vmem((2, 32, 32, TILE), bf16),
+            vmem((4, 32, UNIT, TILE), bf16),
             vmem((TILE, 16 * UNIT), bf16),
             vmem((9, TILE, TILE), f32),
             vmem((128, WIDE), f32),
@@ -442,17 +428,32 @@
             vmem((NROW, 1, 128), f32),
             vmem((NCOL, 1, 128), f32),
             vmem((1, 128), f32),
-            dma((4, LT)), dma((4, LT)), dma((10,)), dma((10,)),
+            dma((len(BANDS), LT)), dma((len(BANDS), LT)), dma((3,)),
             dma((2,)), dma((2,)), dma((6,)), dma((6,)),
-            dma((CHUNKS,)), dma((CHUNKS,)), dma((CHUNKS,)), dma((CHUNKS,)),
+            dma((len(PARTS),)), dma((len(PARTS),)), dma((len(PARTS),)), dma((len(PARTS),)),
             dma((NROW,)), dma((NROW,)), dma((NCOL,)), dma((NCOL,)),
         ],
         compiler_params=pltpu.CompilerParams(
             collective_id=0, has_side_effects=True, vmem_limit_bytes=56 * 1024 * 1024,
         ),
     )(spins_up, uniforms, moments, accept_bar)
-    lattice = jnp.where(weighted > 0, 1.0, -1.0).astype(f32)
-    return lattice, corr[0, :16]
+    block = 128
+    return pl.pallas_call(
+        finish,
+        grid=(ROWS // block,),
+        out_shape=(
+            jax.ShapeDtypeStruct((ROWS, CB), f32),
+            jax.ShapeDtypeStruct((16,), f32),
+        ),
+        in_specs=[
+            pl.BlockSpec((block, CB), lambda i: (i, 0)),
+            pl.BlockSpec((8, 128), lambda i: (0, 0)),
+        ],
+        out_specs=(
+            pl.BlockSpec((block, CB), lambda i: (i, 0)),
+            pl.BlockSpec((16,), lambda i: (0,)),
+        ),
+    )(weighted, corr)
 
 
 def solution(mesh):

time: 73.7 us -> 63.2 us (0.86)
  Pallas kernels: 67.1 us -> 62.4 us
  other arithmetic: 4.6 us -> 0 us
  local copies, waits for them, and re-layouts: 1.19 us -> 0 us
    pallas_call x1, Pallas kernels: 67.1 us -> 57.1 us  [on_device(): pl.pallas_call(kernel, out_shape=(jax.ShapeDtypeStruct((ROWS, CB), bf16),...]
    pallas_call x0 -> x1, Pallas kernels: none -> 5.25 us  [on_device(): pl.pallas_call(finish, grid=(ROWS // block,), out_shape=(jax.ShapeDtypeSt...]
    select_n x1 -> x0, other arithmetic: 4.6 us -> none  [on_device(): lattice = jnp.where(weighted > 0, 1.0, -1.0).astype(f32)]
    squeeze x1 -> x0, local copies, waits for them, and re-layouts: 1.19 us -> none  [on_device(): return (lattice, corr[0, :16])]
where the time goes in v3:
time: 63.2 us; the launch traced here: 63 us
  Pallas kernels  62.4 us (99%)
  between operations  0.64 us (1%)
    pallas_call x1, Pallas kernels, on_device(): pl.pallas_call(kernel, out_shape=(jax.ShapeDtypeStruct((ROWS, CB), bf16),...  57.1 us
    pallas_call x1, Pallas kernels, on_device(): pl.pallas_call(finish, grid=(ROWS // block,), out_shape=(jax.ShapeDtypeSt...  5.25 us

profile of v3, /device:TPU:0, one launch (start us, length us, event | category | flops | bytes accessed | tf_op | source)
XLA Modules:
  0.0 63.0 jit_solution(9898323848467254739)
XLA Ops:
  0.6 57.1 %shard_map.59 = (bf16[640,2048]{1,0:T(8,128)(2,1)}, f32[8,128]{1,0:T(8,128)}) custom-call(s32[640,2048]{1,0:T(8,128)} %su_hbm.1, f32[2,640,2048]{2,1,0:T(8,128)} %u_hbm.1, bf16[640,2048]{1,0:T(8,128)(2,1)} %m_hbm.1, f32[2]{0:T(128)} %bar.1), custom_call_target="tpu_custom_call" | custom-call | tf_op jit(solution)/shard_map/pallas_call | solution.py:402
  57.8 5.3 %shard_map.60 = (f32[640,2048]{1,0:T(8,128)}, f32[16]{0:T(128)}) custom-call(bf16[640,2048]{1,0:T(8,128)(2,1)} %get-tuple-element.4.w_ref, f32[8,128]{1,0:T(8,128)} %get-tuple-element.5.reduced_ref), custom_call_target="tpu_custom_call" | custom-call | tf_op jit(solution)/shard_map/pallas_call | solution.py:441

commit v4 on v3

--- a/solution.py
+++ b/solution.py
@@ -18,9 +18,9 @@
 TILE = 256
 LT = CB // 128
 EDGES = (0, LT - 1)
-BANDS = ((280, 80), (152, 128), (360, 128), (0, 152), (488, 152), (0, 640))
-M_BANDS = ((288, 64), (0, 288), (352, 288))
-PARTS = (32, 64, 64, 64, 64, 32)
+BANDS = ((248, 144), (56, 192), (392, 192), (0, 56), (584, 56), (0, 640))
+M_BANDS = ((256, 128), (0, 256), (384, 256))
+SENDS = ((0, 1, 6), (0, 0, 1), (0, 7, 1), (1, 0, 8), (2, 0, 8), (3, 0, 8), (4, 0, 8), (5, 0, 8))
 SPAN = (UNIT + 2 * HALO) // 8
 PAIRS = SPAN // 2
 MESH = pl.DeviceIdType.MESH
@@ -98,6 +98,9 @@
         hit = (c >= 0) & (c < 4) & (r == 4 * k + c)
         return jnp.where(hit, 1.0, 0.0).astype(bf16)
 
+    for n in range(3):
+        for b in range(5):
+            ht[n, HALO + 128 * b:HALO + 128 * (b + 1), :] = jnp.zeros((128, 128), f32)
     wait_band(5)
 
     for b in range(5):
@@ -160,36 +163,48 @@
     for band in (3, 4):
         start_band(band)
 
-    for side in range(2):
-        col_copy(side).wait_recv()
-
-    for b in range(5):
-        r = HALO + 128 * b
-        src = pl.ds(128 * b, 128)
-        for k in range(3):
-            tile = jnp.zeros((128, 128), f32)
-            for side in range(2):
-                tile = tile + lax.dot_general(
-                    inbox[side, :, src], select(side, k), (((0,), (0,)), ((), ())),
-                    preferred_element_type=f32)
-            ht[k, pl.ds(r, 128), :] = tile
-    for side in range(2):
-        halo_tile_copy(side).start()
+    def column_halos():
+        for side in range(2):
+            col_copy(side).wait_recv()
+
+        for b in range(5):
+            r = HALO + 128 * b
+            src = pl.ds(128 * b, 128)
+            for k in range(3):
+                tile = jnp.zeros((128, 128), f32)
+                for side in range(2):
+                    tile = tile + lax.dot_general(
+                        inbox[side, :, src], select(side, k), (((0,), (0,)), ((), ())),
+                        preferred_element_type=f32)
+                ht[k, pl.ds(r, 128), :] = tile
+        for side in range(2):
+            halo_tile_copy(side).start()
 
     def part(c):
-        return small.at[c // 5] if c in (0, 5) else large.at[c - 1]
-
-    def y_copy(c, ref):
-        return pltpu.make_async_remote_copy(
-            src_ref=ref.at[pl.ds(own, 8)], dst_ref=ref.at[pl.ds(far, 8)],
-            send_sem=ys.at[c], recv_sem=yr.at[c],
+        return small.at[c - 4] if c >= 4 else large.at[c]
+
+    def y_copy(n, ref):
+        _, at, size = SENDS[n]
+        return pltpu.make_async_remote_copy(
+            src_ref=ref.at[pl.ds(own + at, size)], dst_ref=ref.at[pl.ds(far + at, size)],
+            send_sem=ys.at[n], recv_sem=yr.at[n],
             device_id=(row, ycol), device_id_type=MESH)
 
-    def x_copy(c, ref):
-        return pltpu.make_async_remote_copy(
-            src_ref=ref.at[pl.ds(24, 8)], dst_ref=ref.at[pl.ds(8, 8)],
-            send_sem=xs.at[c], recv_sem=xr.at[c],
+    def x_copy(n, ref):
+        _, at, size = SENDS[n]
+        return pltpu.make_async_remote_copy(
+            src_ref=ref.at[pl.ds(24 + at, size)], dst_ref=ref.at[pl.ds(8 + at, size)],
+            send_sem=xs.at[n], recv_sem=xr.at[n],
             device_id=(row, xcol), device_id_type=MESH)
+
+    def send(keep, n):
+        @pl.when(keep == 1)
+        def _():
+            y_copy(n, part(SENDS[n][0])).start()
+
+        @pl.when(keep == 0)
+        def _():
+            x_copy(n, part(SENDS[n][0])).start()
 
     lane = lax.broadcasted_iota(jnp.int32, (8, 128), 1)
     even = lax.rem(lane, 2) == 0
@@ -201,39 +216,39 @@
             ref[0, t] = pltpu.roll(ref[PAIRS, t], 1, 0)
             ref[PAIRS + 1, t] = pltpu.roll(ref[1, t], 7, 0)
 
-    def weigh(c, ref, half, row0, start, count):
-        keep = 1 - lax.rem(half + par, 2)
+    def weigh(ref, keep, row0, start, count, tiles):
         base = own * keep + 24 * (1 - keep)
         for g in range(count // 16):
             at = pl.multiple_of(row0 + start + 16 * g, 16)
-            for t in range(LT):
+            for t in tiles:
                 lanes = pl.ds(128 * t, 128)
                 w = m[pl.ds(at, 16), lanes] * wk[t, HALO + start + 16 * g:HALO + start + 16 * g + 16, :].astype(bf16)
                 ref[base + t // 2, 16 * g:16 * g + 16, 128 * (t % 2):128 * (t % 2 + 1)] = w
                 w_ref[pl.ds(at, 16), lanes] = w
 
-        @pl.when(keep == 1)
+    def unit(k, carry):
+        p = jnp.maximum(k - 2, lax.rem(k, 2))
+        half = lax.rem(p, 2)
+        i = lax.div(p, 2)
+        keep = 1 - lax.rem(half + par, 2)
+        row0 = (256 - UNIT * i) * (1 - half) + (320 + UNIT * i) * half
+
+        @pl.when(k == 2)
         def _():
-            y_copy(c, ref).start()
-
-        @pl.when(keep == 0)
-        def _():
-            x_copy(c, ref).start()
-
-    def unit(k, carry):
-        i = lax.div(k + 1, 2)
-        odd = lax.rem(k, 2)
-        row0 = jnp.minimum(jnp.maximum(288 + UNIT * i * (1 - 2 * odd), 0), ROWS - UNIT)
-
-        for n in range(4):
-            @pl.when(k == 1 + n)
+            column_halos()
+
+        for n in range(2):
+            @pl.when(k == 4 + n)
             def _():
                 wait_band(1 + n)
-                if n < 2:
-                    m_copy(1 + n).wait()
+                m_copy(1 + n).wait()
+
+            @pl.when(k == 8 + n)
+            def _():
+                wait_band(3 + n)
 
         for side in range(2):
-            @pl.when(k == 9 + side)
+            @pl.when(k == 10 + side)
             def _():
                 for cp in row_copies(side):
                     cp.wait_recv()
@@ -289,29 +304,42 @@
                 wk[t, pl.ds(2 * g, 8, stride=SPAN), :] = jnp.where(even, a, b)
                 wk[t, pl.ds(2 * g + 1, 8, stride=SPAN), :] = jnp.where(even, b, a)
 
-        @pl.when(k == 0)
+        @pl.when(k < 2)
         def _():
-            for half in range(2):
-                weigh(0, small.at[0], half, row0, 32 * half, 32)
-
-        @pl.when((k > 0) & (k < 9))
+            weigh(large.at[0], keep, row0, 0, UNIT, range(2, LT - 2))
+            send(keep, 0)
+
+        @pl.when((k >= 2) & (k < 4))
         def _():
-            weigh(i, large.at[i - 1], 1 - odd, row0, 0, UNIT)
-
-        for half in range(2):
-            @pl.when(k == 9 + half)
+            weigh(large.at[0], keep, row0, 0, UNIT, (0, 1, LT - 2, LT - 1))
+            send(keep, 1)
+            send(keep, 2)
+
+        for c in range(1, 4):
+            @pl.when((k >= 2 + 2 * c) & (k < 4 + 2 * c))
             def _():
-                weigh(5, small.at[1], half, row0, 32 * half, 32)
+                weigh(large.at[c], keep, row0, 0, UNIT, range(LT))
+                send(keep, 2 + c)
+
+        for side in range(2):
+            @pl.when(k == 10 + side)
+            def _():
+                for n in range(2):
+                    weigh(small.at[n], keep, row0, 32 * (1 - n if side == 0 else n), 32, range(LT))
+                    send(keep, 6 + n)
 
         return carry
 
     wait_band(0)
     m_copy(0).wait()
-    lax.fori_loop(0, 11, unit, 0)
-
-    def chunk(c, ref, height, opening):
-        y_copy(c, ref).wait_recv()
-        x_copy(c, ref).wait_recv()
+    lax.fori_loop(0, 12, unit, 0)
+
+    def chunk(c, height, opening):
+        ref = part(c)
+        for n, what in enumerate(SENDS):
+            if what[0] == c:
+                y_copy(n, ref).wait_recv()
+                x_copy(n, ref).wait_recv()
         depth = 16 * height
         per = 128 // height
         for n in range(depth // 128):
@@ -322,14 +350,8 @@
             p = jnp.dot(lt[:, 0:depth], right, preferred_element_type=f32)
             prod[o] = p if opening else prod[o] + p
 
-    chunk(0, small.at[0], 32, True)
-
-    def middle(c, carry):
-        chunk(c + 1, large.at[c], UNIT, False)
-        return carry
-
-    lax.fori_loop(0, 4, middle, 0)
-    chunk(5, small.at[1], 32, False)
+    for c in range(6):
+        chunk(c, UNIT if c < 4 else 32, c == 0)
 
     for b in range(16):
         r = 8 * b
@@ -381,24 +403,32 @@
             cp.wait_send()
         halo_tile_copy(side).wait_send()
 
-    for c in range(len(PARTS)):
-        y_copy(c, part(c)).wait_send()
-        x_copy(c, part(c)).wait_send()
+    for n, what in enumerate(SENDS):
+        y_copy(n, part(what[0])).wait_send()
+        x_copy(n, part(what[0])).wait_send()
     for i in range(1, NROW):
         r1_copy(i).wait_send()
     for i in range(1, NCOL):
         r2_copy(i).wait_send()
 
 
-def finish(w_ref, reduced_ref, spins_ref, corr_ref):
-    spins_ref[...] = jnp.where(w_ref[...].astype(jnp.float32) > 0, 1.0, -1.0)
+def finish(w_ref, reduced_ref, spins_hbm, corr_ref, spins, sem):
+    block = 64
+    copies = []
+    for i in range(ROWS // block):
+        rows = pl.ds(block * i, block)
+        spins[rows, :] = jnp.where(w_ref[rows, :].astype(jnp.float32) > 0, 1.0, -1.0)
+        copies.append(pltpu.make_async_copy(spins.at[rows, :], spins_hbm.at[rows, :], sem.at[i]))
+        copies[-1].start()
     corr_ref[...] = reduced_ref[0, :16]
+    for cp in copies:
+        cp.wait()
 
 
 def on_device(spins_up, uniforms, moments, accept_bar):
     f32, bf16 = jnp.float32, jnp.bfloat16
     vmem, dma = pltpu.VMEM, pltpu.SemaphoreType.DMA
-    hbm = pl.BlockSpec(memory_space=pl.ANY)
+    hbm = pl.BlockSpec(memory_space=pltpu.HBM)
     weighted, corr = pl.pallas_call(
         kernel,
         out_shape=(
@@ -430,29 +460,24 @@
             vmem((1, 128), f32),
             dma((len(BANDS), LT)), dma((len(BANDS), LT)), dma((3,)),
             dma((2,)), dma((2,)), dma((6,)), dma((6,)),
-            dma((len(PARTS),)), dma((len(PARTS),)), dma((len(PARTS),)), dma((len(PARTS),)),
+            dma((len(SENDS),)), dma((len(SENDS),)), dma((len(SENDS),)), dma((len(SENDS),)),
             dma((NROW,)), dma((NROW,)), dma((NCOL,)), dma((NCOL,)),
         ],
         compiler_params=pltpu.CompilerParams(
-            collective_id=0, has_side_effects=True, vmem_limit_bytes=56 * 1024 * 1024,
+            collective_id=0, has_side_effects=True, vmem_limit_bytes=50 * 1024 * 1024,
         ),
     )(spins_up, uniforms, moments, accept_bar)
-    block = 128
+    in_vmem = pl.BlockSpec(memory_space=pltpu.VMEM)
     return pl.pallas_call(
         finish,
-        grid=(ROWS // block,),
         out_shape=(
             jax.ShapeDtypeStruct((ROWS, CB), f32),
             jax.ShapeDtypeStruct((16,), f32),
         ),
-        in_specs=[
-            pl.BlockSpec((block, CB), lambda i: (i, 0)),
-            pl.BlockSpec((8, 128), lambda i: (0, 0)),
-        ],
-        out_specs=(
-            pl.BlockSpec((block, CB), lambda i: (i, 0)),
-            pl.BlockSpec((16,), lambda i: (0,)),
-        ),
+        in_specs=[in_vmem, in_vmem],
+        out_specs=(hbm, in_vmem),
+        scratch_shapes=[vmem((ROWS, CB), f32), dma((10,))],
+        compiler_params=pltpu.CompilerParams(vmem_limit_bytes=16 * 1024 * 1024),
     )(weighted, corr)
 
 

time: 63.2 us -> 57.3 us (0.907)
  Pallas kernels: 62.4 us -> 55.9 us
  local copies, waits for them, and re-layouts: 0 us -> 0.65 us
    pallas_call x1, Pallas kernels: 57.1 us -> 52.9 us  [on_device(): pl.pallas_call(kernel, out_shape=(jax.ShapeDtypeStruct((ROWS, CB), bf16),...]
    pallas_call x1, Pallas kernels: 5.25 us -> 2.98 us  [on_device(): pl.pallas_call(finish, out_shape=(jax.ShapeDtypeStruct((ROWS, CB), f32),...]
    unnamed x0 -> x2, local copies, waits for them, and re-layouts: none -> 0.65 us
where the time goes in v4:
time: 57.3 us; the launch traced here: 57.2 us
  Pallas kernels  55.9 us (98%)
  local copies, waits for them, and re-layouts  0.65 us (1%)
  between operations  0.65 us (1%)
    pallas_call x1, Pallas kernels, on_device(): pl.pallas_call(kernel, out_shape=(jax.ShapeDtypeStruct((ROWS, CB), bf16),...  52.9 us
    pallas_call x1, Pallas kernels, on_device(): pl.pallas_call(finish, out_shape=(jax.ShapeDtypeStruct((ROWS, CB), f32),...  2.98 us

profile of v4, /device:TPU:0, one launch (start us, length us, event | category | flops | bytes accessed | tf_op | source)
XLA Modules:
  0.0 57.2 jit_solution(13587927179364751591)
XLA Ops:
  0.6 0.0 copy-start
  0.6 0.6 %copy-done = f32[2]{0:T(128)S(1)} copy-done((f32[2]{0:T(128)S(1)}, f32[2]{0:T(128)}, u32[]{:S(2)}) %copy-start) | copy-done | bytes 32
  1.3 52.9 %shard_map.59 = (bf16[640,2048]{1,0:T(8,128)(2,1)S(1)}, f32[8,128]{1,0:T(8,128)S(1)}) custom-call(s32[640,2048]{1,0:T(8,128)} %su_hbm.1, f32[2,640,2048]{2,1,0:T(8,128)} %u_hbm.1, bf16[640,2048]{1,0:T(8,128)(2,1)} %m_hbm.1, f32[2]{0:T(128)S(1)} %copy-done), custom_call_target="tpu_custom_call" | custom-call | tf_op jit(solution)/shard_map/pallas_call | solution.py:432
  54.2 3.0 %shard_map.60 = (f32[640,2048]{1,0:T(8,128)}, f32[16]{0:T(128)}) custom-call(bf16[640,2048]{1,0:T(8,128)(2,1)S(1)} %get-tuple-element.4.w_ref, f32[8,128]{1,0:T(8,128)S(1)} %get-tuple-element.5.reduced_ref), custom_call_target="tpu_custom_call" | custom-call | tf_op jit(solution)/shard_map/pallas_call | solution.py:471
Async XLA Ops:
  0.6 0.7 %copy-start = (f32[2]{0:T(128)S(1)}, f32[2]{0:T(128)}, u32[]{:S(2)}) copy-start(f32[2]{0:T(128)} %bar.1) | copy-start | bytes 28

commit v5 on v4

--- a/solution.py
+++ b/solution.py
@@ -18,9 +18,13 @@
 TILE = 256
 LT = CB // 128
 EDGES = (0, LT - 1)
-BANDS = ((248, 144), (56, 192), (392, 192), (0, 56), (584, 56), (0, 640))
-M_BANDS = ((256, 128), (0, 256), (384, 256))
-SENDS = ((0, 1, 6), (0, 0, 1), (0, 7, 1), (1, 0, 8), (2, 0, 8), (3, 0, 8), (4, 0, 8), (5, 0, 8))
+BANDS = ((216, 208), (88, 128), (424, 128), (0, 88), (552, 88), (0, 640))
+M_BANDS = ((224, 192), (0, 224), (416, 224))
+SENDS = (
+    (0, 1, 6), (1, 1, 6), (0, 0, 1), (0, 7, 1), (1, 0, 1), (1, 7, 1),
+    (2, 0, 8), (3, 0, 8), (4, 0, 8), (5, 0, 8), (6, 0, 8),
+)
+HEIGHTS = (32, 64, 64, 64, 64, 16, 16)
 SPAN = (UNIT + 2 * HALO) // 8
 PAIRS = SPAN // 2
 MESH = pl.DeviceIdType.MESH
@@ -28,7 +32,7 @@
 
 def kernel(
     su_hbm, u_hbm, m_hbm, bar, w_ref, corr_ref,
-    su, u, hu, hs, m, ht, c0, c1, wk, small, large, lt, prod, fold, outbox, inbox, vb, rs1, rs2, sb,
+    su, u, hu, hs, m, ht, c0, c1, wk, small, large, tiny, lt, prod, fold, outbox, inbox, vb, rs1, rs2, sb,
     u_sem, s_sem, m_sem, col_send, col_recv,
     row_send, row_recv, ys, yr, xs, xr, r1s, r1r, r2s, r2r,
 ):
@@ -160,8 +164,6 @@
     for band in (1, 2):
         start_band(band)
         m_copy(band).start()
-    for band in (3, 4):
-        start_band(band)
 
     def column_halos():
         for side in range(2):
@@ -181,7 +183,7 @@
             halo_tile_copy(side).start()
 
     def part(c):
-        return small.at[c - 4] if c >= 4 else large.at[c]
+        return small if c == 0 else large.at[c - 1] if c < 5 else tiny.at[c - 5]
 
     def y_copy(n, ref):
         _, at, size = SENDS[n]
@@ -227,28 +229,30 @@
                 w_ref[pl.ds(at, 16), lanes] = w
 
     def unit(k, carry):
-        p = jnp.maximum(k - 2, lax.rem(k, 2))
-        half = lax.rem(p, 2)
-        i = lax.div(p, 2)
-        keep = 1 - lax.rem(half + par, 2)
-        row0 = (256 - UNIT * i) * (1 - half) + (320 + UNIT * i) * half
-
-        @pl.when(k == 2)
+        p = k - 3 * jnp.minimum(lax.div(k, 3), 1)
+        odd = lax.rem(p, 2)
+        i = lax.div(p + 1, 2)
+        keep = 1 - lax.rem(1 - odd + par, 2)
+        row0 = jnp.minimum(jnp.maximum(288 + UNIT * i * (1 - 2 * odd), 0), ROWS - UNIT)
+
+        @pl.when(k == 3)
         def _():
+            for n in range(2):
+                start_band(3 + n)
             column_halos()
 
         for n in range(2):
-            @pl.when(k == 4 + n)
+            @pl.when(k == 6 + n)
             def _():
                 wait_band(1 + n)
                 m_copy(1 + n).wait()
 
-            @pl.when(k == 8 + n)
+            @pl.when(k == 10 + n)
             def _():
                 wait_band(3 + n)
 
         for side in range(2):
-            @pl.when(k == 10 + side)
+            @pl.when(k == 12 + side)
             def _():
                 for cp in row_copies(side):
                     cp.wait_recv()
@@ -304,35 +308,42 @@
                 wk[t, pl.ds(2 * g, 8, stride=SPAN), :] = jnp.where(even, a, b)
                 wk[t, pl.ds(2 * g + 1, 8, stride=SPAN), :] = jnp.where(even, b, a)
 
-        @pl.when(k < 2)
-        def _():
-            weigh(large.at[0], keep, row0, 0, UNIT, range(2, LT - 2))
-            send(keep, 0)
-
-        @pl.when((k >= 2) & (k < 4))
-        def _():
-            weigh(large.at[0], keep, row0, 0, UNIT, (0, 1, LT - 2, LT - 1))
-            send(keep, 1)
-            send(keep, 2)
+        inner, edges = range(2, LT - 2), (0, 1, LT - 2, LT - 1)
+        for late in range(2):
+            tiles = edges if late else inner
+
+            @pl.when(k == 3 * late)
+            def _():
+                for half in range(2):
+                    kept = 1 - lax.rem(half + par, 2)
+                    weigh(small, kept, row0, 32 * half, 32, tiles)
+                    for n in (2, 3) if late else (0,):
+                        send(kept, n)
+
+            @pl.when((k >= 1 + 3 * late) & (k < 3 + 3 * late))
+            def _():
+                weigh(large.at[0], keep, row0, 0, UNIT, tiles)
+                for n in (4, 5) if late else (1,):
+                    send(keep, n)
 
         for c in range(1, 4):
-            @pl.when((k >= 2 + 2 * c) & (k < 4 + 2 * c))
+            @pl.when((k >= 4 + 2 * c) & (k < 6 + 2 * c))
             def _():
                 weigh(large.at[c], keep, row0, 0, UNIT, range(LT))
-                send(keep, 2 + c)
+                send(keep, 5 + c)
 
         for side in range(2):
-            @pl.when(k == 10 + side)
+            @pl.when(k == 12 + side)
             def _():
                 for n in range(2):
-                    weigh(small.at[n], keep, row0, 32 * (1 - n if side == 0 else n), 32, range(LT))
-                    send(keep, 6 + n)
+                    weigh(tiny.at[n], keep, row0, 16 * (1 - n) if side == 0 else 32 + 16 * n, 16, range(LT))
+                    send(keep, 9 + n)
 
         return carry
 
     wait_band(0)
     m_copy(0).wait()
-    lax.fori_loop(0, 12, unit, 0)
+    lax.fori_loop(0, 14, unit, 0)
 
     def chunk(c, height, opening):
         ref = part(c)
@@ -350,8 +361,8 @@
             p = jnp.dot(lt[:, 0:depth], right, preferred_element_type=f32)
             prod[o] = p if opening else prod[o] + p
 
-    for c in range(6):
-        chunk(c, UNIT if c < 4 else 32, c == 0)
+    for c, height in enumerate(HEIGHTS):
+        chunk(c, height, c == 0)
 
     for b in range(16):
         r = 8 * b
@@ -447,8 +458,9 @@
             vmem((PAIRS + 2, LT + 1, 8, 128), f32),
             vmem((PAIRS + 2, LT + 1, 8, 128), f32),
             vmem((LT, UNIT + 16, 128), f32),
-            vmem((2, 32, 32, TILE), bf16),
+            vmem((32, 32, TILE), bf16),
             vmem((4, 32, UNIT, TILE), bf16),
+            vmem((2, 32, 16, TILE), bf16),
             vmem((TILE, 16 * UNIT), bf16),
             vmem((9, TILE, TILE), f32),
             vmem((128, WIDE), f32),

time: 57.3 us -> 57.4 us (level)
  no operation moved by 1% of the time
where the time goes in v5:
time: 57.4 us; the launch traced here: 57.3 us
  Pallas kernels  56 us (98%)
  local copies, waits for them, and re-layouts  0.65 us (1%)
  between operations  0.65 us (1%)
    pallas_call x1, Pallas kernels, on_device(): pl.pallas_call(kernel, out_shape=(jax.ShapeDtypeStruct((ROWS, CB), bf16),...  53 us
    pallas_call x1, Pallas kernels, on_device(): pl.pallas_call(finish, out_shape=(jax.ShapeDtypeStruct((ROWS, CB), f32),...  2.98 us

profile of v5, /device:TPU:0, one launch (start us, length us, event | category | flops | bytes accessed | tf_op | source)
XLA Modules:
  0.0 57.3 jit_solution(15145762225905612664)
XLA Ops:
  0.6 0.0 copy-start
  0.6 0.6 %copy-done = f32[2]{0:T(128)S(1)} copy-done((f32[2]{0:T(128)S(1)}, f32[2]{0:T(128)}, u32[]{:S(2)}) %copy-start) | copy-done | bytes 32
  1.3 53.0 %shard_map.59 = (bf16[640,2048]{1,0:T(8,128)(2,1)S(1)}, f32[8,128]{1,0:T(8,128)S(1)}) custom-call(s32[640,2048]{1,0:T(8,128)} %su_hbm.1, f32[2,640,2048]{2,1,0:T(8,128)} %u_hbm.1, bf16[640,2048]{1,0:T(8,128)(2,1)} %m_hbm.1, f32[2]{0:T(128)S(1)} %copy-done), custom_call_target="tpu_custom_call" | custom-call | tf_op jit(solution)/shard_map/pallas_call | solution.py:443
  54.3 3.0 %shard_map.60 = (f32[640,2048]{1,0:T(8,128)}, f32[16]{0:T(128)}) custom-call(bf16[640,2048]{1,0:T(8,128)(2,1)S(1)} %get-tuple-element.4.w_ref, f32[8,128]{1,0:T(8,128)S(1)} %get-tuple-element.5.reduced_ref), custom_call_target="tpu_custom_call" | custom-call | tf_op jit(solution)/shard_map/pallas_call | solution.py:483
Async XLA Ops:
  0.6 0.7 %copy-start = (f32[2]{0:T(128)S(1)}, f32[2]{0:T(128)}, u32[]{:S(2)}) copy-start(f32[2]{0:T(128)} %bar.1) | copy-start | bytes 28

commit v6 on v5

--- a/solution.py
+++ b/solution.py
@@ -27,14 +27,18 @@
 HEIGHTS = (32, 64, 64, 64, 64, 16, 16)
 SPAN = (UNIT + 2 * HALO) // 8
 PAIRS = SPAN // 2
+ORDER = sorted(
+    ((i, j) for i in range(NROW) for j in range(NCOL) if i or j),
+    key=lambda e: (-(2 - abs(2 - e[0] // 2 % 4)) - 2 * (e[0] // 8) - (2 - abs(2 - e[1] // 2)), e),
+)
 MESH = pl.DeviceIdType.MESH
 
 
 def kernel(
     su_hbm, u_hbm, m_hbm, bar, w_ref, corr_ref,
-    su, u, hu, hs, m, ht, c0, c1, wk, small, large, tiny, lt, prod, fold, outbox, inbox, vb, rs1, rs2, sb,
+    su, u, hu, hs, m, ht, c0, c1, wk, small, large, tiny, lt, prod, fold, outbox, inbox, vb, gathered,
     u_sem, s_sem, m_sem, col_send, col_recv,
-    row_send, row_recv, ys, yr, xs, xr, r1s, r1r, r2s, r2r,
+    row_send, row_recv, ys, yr, xs, xr, all_send, all_recv, entered,
 ):
     f32, bf16 = jnp.float32, jnp.bfloat16
     row = lax.axis_index("row")
@@ -125,6 +129,10 @@
             outbox[side, :, dst] = msg.astype(bf16)
 
     pl.semaphore_wait(barrier, NROW + NCOL - 2)
+    for i in range(1, NCOL):
+        pl.semaphore_signal(
+            entered, inc=1, device_id=(row, lax.rem(col + i, NCOL)), device_id_type=MESH
+        )
 
     def col_copy(side):
         return pltpu.make_async_remote_copy(
@@ -380,30 +388,23 @@
     for i in range(NROW):
         vb[i] = v[0:1, 128 * i:128 * (i + 1)]
 
-    def r1_copy(i):
-        to = lax.rem(row + i, NROW)
-        return pltpu.make_async_remote_copy(
-            src_ref=vb.at[to], dst_ref=rs1.at[i], send_sem=r1s.at[i], recv_sem=r1r.at[i],
-            device_id=(to, col), device_id_type=MESH)
-
-    for i in range(1, NROW):
-        r1_copy(i).start()
-    total = vb[row]
-    for i in range(1, NROW):
-        r1_copy(i).wait_recv()
-        total = total + rs1[i]
-    sb[...] = total
-
-    def r2_copy(i):
-        return pltpu.make_async_remote_copy(
-            src_ref=sb, dst_ref=rs2.at[i], send_sem=r2s.at[i], recv_sem=r2r.at[i],
-            device_id=(row, lax.rem(col + i, NCOL)), device_id_type=MESH)
-
-    for i in range(1, NCOL):
-        r2_copy(i).start()
-    for i in range(1, NCOL):
-        r2_copy(i).wait_recv()
-        total = total + rs2[i]
+    to_row = [lax.rem(row + i, NROW) for i in range(NROW)]
+    to_col = [lax.rem(col + i, NCOL) for i in range(NCOL)]
+    pl.semaphore_wait(entered, NCOL - 1)
+    for i, j in ORDER:
+        pltpu.make_async_remote_copy(
+            src_ref=vb.at[to_row[i]], dst_ref=gathered.at[NCOL * i + j],
+            send_sem=all_send.at[0], recv_sem=all_recv.at[0],
+            device_id=(to_row[i], to_col[j]), device_id_type=MESH).start()
+    others = gathered.at[pl.ds(1, NROW * NCOL - 1)]
+    every = pltpu.make_async_remote_copy(
+        src_ref=others, dst_ref=others, send_sem=all_send.at[0], recv_sem=all_recv.at[0],
+        device_id=(row, right), device_id_type=MESH)
+    every.wait_recv()
+    sums = [vb[row]] + [gathered[i] for i in range(1, 8)]
+    for i in range(8, NROW * NCOL):
+        sums[i % 8] = sums[i % 8] + gathered[i]
+    total = sum(sums[1:], sums[0])
     total = total * (1.0 / math.sqrt(ROWS * NROW * CB * NCOL))
     total = pltpu.roll(jnp.broadcast_to(total, (8, 128)), lax.rem(128 - 16 * col, 128), 1)
     corr_ref[...] = total
@@ -417,10 +418,7 @@
     for n, what in enumerate(SENDS):
         y_copy(n, part(what[0])).wait_send()
         x_copy(n, part(what[0])).wait_send()
-    for i in range(1, NROW):
-        r1_copy(i).wait_send()
-    for i in range(1, NCOL):
-        r2_copy(i).wait_send()
+    every.wait_send()
 
 
 def finish(w_ref, reduced_ref, spins_hbm, corr_ref, spins, sem):
@@ -467,13 +465,11 @@
             vmem((2, 16, ROWS), bf16),
             vmem((2, 16, ROWS), bf16),
             vmem((NROW, 1, 128), f32),
-            vmem((NROW, 1, 128), f32),
-            vmem((NCOL, 1, 128), f32),
-            vmem((1, 128), f32),
+            vmem((NROW * NCOL, 1, 128), f32),
             dma((len(BANDS), LT)), dma((len(BANDS), LT)), dma((3,)),
             dma((2,)), dma((2,)), dma((6,)), dma((6,)),
             dma((len(SENDS),)), dma((len(SENDS),)), dma((len(SENDS),)), dma((len(SENDS),)),
-            dma((NROW,)), dma((NROW,)), dma((NCOL,)), dma((NCOL,)),
+            dma((1,)), dma((1,)), pltpu.SemaphoreType.REGULAR,
         ],
         compiler_params=pltpu.CompilerParams(
             collective_id=0, has_side_effects=True, vmem_limit_bytes=50 * 1024 * 1024,

time: 57.4 us -> 55.8 us (0.972); the launches traced: 57.3 us -> 54.9 us
  Pallas kernels: 56 us -> 53.6 us
    pallas_call x1, Pallas kernels: 53 us -> 50.7 us  [on_device(): pl.pallas_call(kernel, out_shape=(jax.ShapeDtypeStruct((ROWS, CB), bf16),...]
where the time goes in v6:
time: 55.8 us; the launch traced here: 54.9 us
  Pallas kernels  53.6 us (96%)
  local copies, waits for them, and re-layouts  0.65 us (1%)
  between operations  0.65 us (1%)
    pallas_call x1, Pallas kernels, on_device(): pl.pallas_call(kernel, out_shape=(jax.ShapeDtypeStruct((ROWS, CB), bf16),...  50.7 us
    pallas_call x1, Pallas kernels, on_device(): pl.pallas_call(finish, out_shape=(jax.ShapeDtypeStruct((ROWS, CB), f32),...  2.98 us

profile of v6, /device:TPU:0, one launch (start us, length us, event | category | flops | bytes accessed | tf_op | source)
XLA Modules:
  0.0 54.9 jit_solution(15053819247559159146)
XLA Ops:
  0.6 0.0 copy-start
  0.6 0.6 %copy-done = f32[2]{0:T(128)S(1)} copy-done((f32[2]{0:T(128)S(1)}, f32[2]{0:T(128)}, u32[]{:S(2)}) %copy-start) | copy-done | bytes 32
  1.3 50.7 %shard_map.59 = (bf16[640,2048]{1,0:T(8,128)(2,1)S(1)}, f32[8,128]{1,0:T(8,128)S(1)}) custom-call(s32[640,2048]{1,0:T(8,128)} %su_hbm.1, f32[2,640,2048]{2,1,0:T(8,128)} %u_hbm.1, bf16[640,2048]{1,0:T(8,128)(2,1)} %m_hbm.1, f32[2]{0:T(128)S(1)} %copy-done), custom_call_target="tpu_custom_call" | custom-call | tf_op jit(solution)/shard_map/pallas_call | solution.py:441
  51.9 3.0 %shard_map.60 = (f32[640,2048]{1,0:T(8,128)}, f32[16]{0:T(128)}) custom-call(bf16[640,2048]{1,0:T(8,128)(2,1)S(1)} %get-tuple-element.4.w_ref, f32[8,128]{1,0:T(8,128)S(1)} %get-tuple-element.5.reduced_ref), custom_call_target="tpu_custom_call" | custom-call | tf_op jit(solution)/shard_map/pallas_call | solution.py:479
Async XLA Ops:
  0.6 0.7 %copy-start = (f32[2]{0:T(128)S(1)}, f32[2]{0:T(128)}, u32[]{:S(2)}) copy-start(f32[2]{0:T(128)} %bar.1) | copy-start | bytes 28

commit v7 on v6

--- a/solution.py
+++ b/solution.py
@@ -422,16 +422,26 @@
 
 
 def finish(w_ref, reduced_ref, spins_hbm, corr_ref, spins, sem):
-    block = 64
-    copies = []
-    for i in range(ROWS // block):
-        rows = pl.ds(block * i, block)
+    block = 32
+
+    def copy(i):
+        rows = pl.ds(pl.multiple_of(block * i, block), block)
+        return pltpu.make_async_copy(spins.at[rows, :], spins_hbm.at[rows, :], sem.at[i])
+
+    def write(i, carry):
+        rows = pl.ds(pl.multiple_of(block * i, block), block)
         spins[rows, :] = jnp.where(w_ref[rows, :].astype(jnp.float32) > 0, 1.0, -1.0)
-        copies.append(pltpu.make_async_copy(spins.at[rows, :], spins_hbm.at[rows, :], sem.at[i]))
-        copies[-1].start()
+        copy(i).start()
+        return carry
+
+    lax.fori_loop(0, ROWS // block, write, 0)
     corr_ref[...] = reduced_ref[0, :16]
-    for cp in copies:
-        cp.wait()
+
+    def drain(i, carry):
+        copy(i).wait()
+        return carry
+
+    lax.fori_loop(0, ROWS // block, drain, 0)
 
 
 def on_device(spins_up, uniforms, moments, accept_bar):
@@ -484,7 +494,7 @@
         ),
         in_specs=[in_vmem, in_vmem],
         out_specs=(hbm, in_vmem),
-        scratch_shapes=[vmem((ROWS, CB), f32), dma((10,))],
+        scratch_shapes=[vmem((ROWS, CB), f32), dma((20,))],
         compiler_params=pltpu.CompilerParams(vmem_limit_bytes=16 * 1024 * 1024),
     )(weighted, corr)
 

time: 55.8 us -> 55.8 us (level)
  no operation moved by 1% of the time
where the time goes in v7:
time: 55.8 us; the launch traced here: 55 us
  Pallas kernels  53.7 us (96%)
  local copies, waits for them, and re-layouts  0.65 us (1%)
  between operations  0.65 us (1%)
    pallas_call x1, Pallas kernels, on_device(): pl.pallas_call(kernel, out_shape=(jax.ShapeDtypeStruct((ROWS, CB), bf16),...  50.7 us
    pallas_call x1, Pallas kernels, on_device(): pl.pallas_call(finish, out_shape=(jax.ShapeDtypeStruct((ROWS, CB), f32),...  3.03 us

profile of v7, /device:TPU:0, one launch (start us, length us, event | category | flops | bytes accessed | tf_op | source)
XLA Modules:
  0.0 55.0 jit_solution(2486223277337189510)
XLA Ops:
  0.6 0.0 copy-start
  0.6 0.6 %copy-done = f32[2]{0:T(128)S(1)} copy-done((f32[2]{0:T(128)S(1)}, f32[2]{0:T(128)}, u32[]{:S(2)}) %copy-start) | copy-done | bytes 32
  1.3 50.7 %shard_map.59 = (bf16[640,2048]{1,0:T(8,128)(2,1)S(1)}, f32[8,128]{1,0:T(8,128)S(1)}) custom-call(s32[640,2048]{1,0:T(8,128)} %su_hbm.1, f32[2,640,2048]{2,1,0:T(8,128)} %u_hbm.1, bf16[640,2048]{1,0:T(8,128)(2,1)} %m_hbm.1, f32[2]{0:T(128)S(1)} %copy-done), custom_call_target="tpu_custom_call" | custom-call | tf_op jit(solution)/shard_map/pallas_call | solution.py:451
  51.9 3.0 %shard_map.60 = (f32[640,2048]{1,0:T(8,128)}, f32[16]{0:T(128)}) custom-call(bf16[640,2048]{1,0:T(8,128)(2,1)S(1)} %get-tuple-element.4.w_ref, f32[8,128]{1,0:T(8,128)S(1)} %get-tuple-element.5.reduced_ref), custom_call_target="tpu_custom_call" | custom-call | tf_op jit(solution)/shard_map/pallas_call | solution.py:489
Async XLA Ops:
  0.6 0.7 %copy-start = (f32[2]{0:T(128)S(1)}, f32[2]{0:T(128)}, u32[]{:S(2)}) copy-start(f32[2]{0:T(128)} %bar.1) | copy-start | bytes 28
